TPU v7x, 8 devices: a whole 2x2x1 slice. The times are simulated.
8 devices in a mesh: mat: 1 (over z), col: 2 (over y), row: 4 (over x, core).
Axes of the slice: x: 2, y: 2, z: 1, core: 2. Of those that a mesh axis runs over, the one named last changes fastest.
Arguments:
- a_mat: float32 [8192, 4, 192], P(('mat', 'row'), 'col')
Outputs:
- output 1: float32 [8192, 4, 192], P(('mat', 'row'), 'col')
- output 2: float32 [4, 192], P(('mat', 'col'))
- output 3: float32 [4, 192, 192], P(('mat', 'col'))
All inputs are finite; a program needn't handle non-finite values.
Results may differ from a plain program's by a relative error of at most 0.001.
Values sent between devices are 32-bit elements.
A program may use at most 1 GiB of HBM per device.

v0:
```python
import functools

import jax
import jax.numpy as jnp
from jax import lax
from jax.experimental import pallas as pl
from jax.experimental.pallas import tpu as pltpu
from jax.sharding import PartitionSpec as P

FULL_PREC = lax.Precision.HIGHEST
SUB = 64
LANES = 128
MIN_PIVOT = 1e-3
MAX_COEF = 64.0


def dot(a, b, ca=1, cb=0):
    return lax.dot_general(a, b, (((ca,), (cb,)), ((), ())), precision=FULL_PREC, preferred_element_type=jnp.float32)


def factor_block(g, b, r_ref, x_ref):
    n = g.shape[0]
    nt = n // 8
    zero = jnp.zeros((n, LANES - n), jnp.float32)
    eye = (lax.broadcasted_iota(jnp.int32, (n, n), 0) == lax.broadcasted_iota(jnp.int32, (n, n), 1)).astype(jnp.float32)
    gp = jnp.concatenate([g, zero], axis=1)
    bp = jnp.concatenate([b, eye], axis=1)
    gt = [gp[8 * i:8 * i + 8] for i in range(nt)]
    bt = [bp[8 * i:8 * i + 8] for i in range(nt)]
    lane = lax.broadcasted_iota(jnp.int32, (8, LANES), 1)
    row8 = lax.broadcasted_iota(jnp.int32, (8, LANES), 0)
    lane1 = lane[0:1]
    tau_row = jnp.zeros((1, LANES), jnp.float32)
    piv_row = jnp.zeros((1, LANES), jnp.float32)
    sgn_row = jnp.zeros((1, LANES), jnp.float32)
    full = (8, LANES)

    def row_of(tile, r):
        return jnp.broadcast_to(tile[r:r + 1, :], full)

    for q in range(nt):
        eg = [[jnp.broadcast_to(gt[i][:, 8 * q + c:8 * q + c + 1], full) for c in range(8)] for i in range(nt)]
        eb = [[jnp.broadcast_to(bt[i][:, 8 * q + c:8 * q + c + 1], full) for c in range(8)] for i in range(nt)]
        for r in range(8):
            k = 8 * q + r
            at_row = row8 == r
            right = lane > k
            here = lane == k
            piv = row_of(eg[q][r], r)
            inv = 1.0 / piv
            root = jnp.sqrt(piv)
            unit = root * inv
            g_cols = [row_of(eg[q][c], r) for c in range(r + 1, 8)]
            row_g = row_of(gt[q], r)
            g_right = jnp.where(right, row_g, 0.0)
            g_keep = jnp.where(here, inv, g_right)
            alpha = row_of(eb[q][r], r)
            s = jnp.where(alpha >= 0.0, 1.0, -1.0)
            beta = -s * root
            xkk = alpha - beta
            rx = 1.0 / xkk
            su = s * unit
            x_cols = [row_of(eb[q][c], r) + su * g_cols[c - r - 1] for c in range(r + 1, 8)]
            row_b = row_of(bt[q], r)
            r_row = -(su * g_right)
            x_right = jnp.where(right, row_b - r_row, 0.0)
            x_keep = jnp.where(here, rx, jnp.where(right, x_right, row_b))
            for i in range(nt):
                m = eg[i][r] * inv
                wide = jnp.where(here, m, gt[i] - m * g_right)
                if i == q:
                    wide = jnp.where(at_row, g_keep, wide)
                    m = jnp.where(at_row, 0.0, m)
                gt[i] = wide
                for c in range(r + 1, 8):
                    eg[i][c] = eg[i][c] - m * g_cols[c - r - 1]
            for i in range(nt):
                m = eb[i][r] * rx
                wide = jnp.where(here, m, bt[i] - m * x_right)
                if i == q:
                    wide = jnp.where(at_row, x_keep, wide)
                bt[i] = wide
                for c in range(r + 1, 8):
                    new = eb[i][c] - m * x_cols[c - r - 1]
                    if i == q:
                        new = jnp.where(at_row, x_cols[c - r - 1], new)
                    eb[i][c] = new
            r_ref[k:k + 1, :] = jnp.where(here, beta, r_row)[0:1]
            x_ref[k:k + 1, :] = jnp.where(here, xkk, x_right)[0:1]
            here1 = lane1 == k
            tau_row = jnp.where(here1, ((beta - alpha) / beta)[0:1], tau_row)
            piv_row = jnp.where(here1, piv[0:1], piv_row)
            sgn_row = jnp.where(here1, beta[0:1], sgn_row)
    mg = jnp.concatenate(gt, axis=0)[:, :n]
    mb = jnp.concatenate(bt, axis=0)[:, :n]
    ri = lax.broadcasted_iota(jnp.int32, (n, n), 0)
    ci = lax.broadcasted_iota(jnp.int32, (n, n), 1)
    x_inv_d = jnp.sum(jnp.where(ri == ci, mb, 0.0), axis=1, keepdims=True)
    g_inv_d = jnp.sum(jnp.where(ri == ci, mg, 0.0), axis=1, keepdims=True)
    x_inv = jnp.where(ri == ci, mb, jnp.where(ri < ci, -mb * x_inv_d, 0.0))
    u_inv = jnp.where(ri == ci, mg, jnp.where(ri < ci, -mg * g_inv_d, 0.0))
    r_inv = u_inv * sgn_row[:, :n]
    v = jnp.where(ri > ci, mb, 0.0)
    return v, x_inv, r_inv, tau_row[:, :n], piv_row[:, :n]


def factor_kernel(count, width, place, f_in, h_in, top_out, xi_out, t_ref, tau_ref, ok_ref, top_ref, xi_ref, g_ref, w_ref, x_ref, rb_ref, xb_ref, gs, bs, ri_s, vi_s, xi_s, rs, xs, vs, dg_ref, dc_ref, tau_s):
    subs = width // SUB
    ri = lax.broadcasted_iota(jnp.int32, (width, width), 0)
    ci = lax.broadcasted_iota(jnp.int32, (width, width), 1)
    for i in range(count):
        qi, si = i % 2, i // 2 * width
        for j in range(count):
            qj, sj = j % 2, j // 2 * width
            w_ref[i, j] = h_in[qj, sj:sj + width, i * width:(i + 1) * width].T
            if i <= j:
                if qi == qj:
                    g_ref[i, j] = f_in[qi, si:si + width, sj:sj + width]
                elif qi == 0:
                    g_ref[i, j] = f_in[2, si:si + width, sj:sj + width]
                else:
                    g_ref[i, j] = f_in[2, sj:sj + width, si:si + width].T
        dg_ref[i] = jnp.sum(jnp.where(ri == ci, g_ref[i, i], 0.0), axis=0, keepdims=True)
        dc_ref[i] = jnp.sqrt(jnp.sum(jnp.where(ri == ci, g_ref[i, i], 0.0), axis=1, keepdims=True))
    q = place[0]
    xi_out[...] = jnp.zeros_like(xi_out)

    def panel(j, bad):
        gs[...] = g_ref[j, j]
        bs[...] = w_ref[j, j]
        diag0 = dg_ref[j]
        for ref in (rs, xs, vs, ri_s, vi_s, xi_s):
            ref[...] = jnp.zeros_like(ref)
        for s in range(subs):
            c0, c1 = s * SUB, (s + 1) * SUB
            v, x_inv, r_inv, tau, piv = factor_block(gs[c0:c1, c0:c1], bs[c0:c1, c0:c1], rb_ref, xb_ref)
            v_inv = xb_ref[:, SUB:2 * SUB]
            rs[c0:c1, c0:c1] = rb_ref[:, :SUB]
            xs[c0:c1, c0:c1] = xb_ref[:, :SUB]
            vs[c0:c1, c0:c1] = v
            ri_s[c0:c1, c0:c1] = r_inv
            xi_s[c0:c1, c0:c1] = x_inv
            vi_s[c0:c1, c0:c1] = v_inv
            tau_s[0:1, c0:c1] = tau
            bad = jnp.maximum(bad, jnp.max(jnp.where(piv > MIN_PIVOT * diag0[:, c0:c1], 0.0, 1.0)))
            if s + 1 < subs:
                r_row = dot(r_inv, gs[c0:c1, c1:], 0, 0)
                x_row = dot(v_inv, bs[c0:c1, c1:] - r_row)
                v_col = dot(bs[c1:, c0:c1], x_inv)
                rs[c0:c1, c1:] = r_row
                xs[c0:c1, c1:] = x_row
                vs[c1:, c0:c1] = v_col
                gs[c1:, c1:] -= dot(r_row, r_row, 0, 0)
                bs[c1:, c1:] -= dot(v_col, x_row)
            if s > 0:
                xi_s[:c0, c0:c1] = -dot(xi_s[:c0, :c0], dot(xs[:c0, c0:c1], x_inv))
                ri_s[:c0, c0:c1] = -dot(ri_s[:c0, :c0], dot(rs[:c0, c0:c1], r_inv))
                vi_s[c0:c1, :c0] = -dot(dot(v_inv, vs[c0:c1, :c0]), vi_s[:c0, :c0])
        x_inv, r_inv, v_inv = xi_s[...], ri_s[...], vi_s[...]
        xi_ref[j, j] = x_inv
        top_ref[j, j] = rs[...] + vs[...]

        def right(t, carry):
            r_row = dot(r_inv, g_ref[j, t], 0, 0)
            top_ref[j, t] = r_row
            x_ref[j, t] = dot(v_inv, w_ref[j, t] - r_row)
            return carry

        lax.fori_loop(j + 1, count, right, 0)

        def below(i, carry):
            v_col = dot(w_ref[i, j], x_inv)
            top_ref[i, j] = v_col

            def upd_w(t, c):
                w_ref[i, t] -= dot(v_col, x_ref[j, t])
                return c

            lax.fori_loop(j + 1, count, upd_w, 0)
            r_i = top_ref[j, i]

            def upd_g(t, c):
                g_ref[i, t] -= dot(r_i, top_ref[j, t], 0, 0)
                return c

            lax.fori_loop(i, count, upd_g, 0)
            return carry

        lax.fori_loop(j + 1, count, below, 0)

        def inv_col(i, carry):
            def add(m, acc):
                return acc + dot(xi_ref[i, m], x_ref[m, j])

            xi_ref[i, j] = -dot(lax.fori_loop(i, j, add, jnp.zeros((width, width), jnp.float32)), x_inv)
            return carry

        lax.fori_loop(0, j, inv_col, 0)

        def coef(i, acc):
            return acc + jnp.sum(dc_ref[i] * jnp.abs(xi_ref[i, j]), axis=0, keepdims=True)

        size = lax.fori_loop(0, j + 1, coef, jnp.zeros((1, width), jnp.float32))
        slot = j // 2

        @pl.when(j % 2 == q)
        def _():
            t_ref[slot] = -dot(dot(xs[...], r_inv), v_inv, 1, 1)
            tau_ref[slot] = tau_s[...]
            for i in range(count):
                top_out[slot, i] = top_ref[i, j]

            def put(i, c):
                xi_out[slot, 2 * (i // 2) + (i + q) % 2] = xi_ref[i, j]
                return c

            lax.fori_loop(0, j + 1, put, 0)

        return jnp.maximum(bad, jnp.max(jnp.where(size < MAX_COEF, 0.0, 1.0)))

    bad = lax.fori_loop(0, count, panel, jnp.float32(0.0))
    ok_ref[...] = jnp.full(ok_ref.shape, bad, jnp.float32)


def factor_call(place, f, h, count, width):
    f32 = jnp.float32
    blocks = jax.ShapeDtypeStruct((2, count, width, width), f32)
    vmem = pl.BlockSpec(memory_space=pltpu.VMEM)
    sq = pltpu.VMEM((width, width), f32)
    return pl.pallas_call(
        functools.partial(factor_kernel, count, width),
        out_shape=(blocks, blocks, jax.ShapeDtypeStruct((2, width, width), f32), jax.ShapeDtypeStruct((2, 1, width), f32), jax.ShapeDtypeStruct((8, 128), f32)),
        in_specs=[pl.BlockSpec(memory_space=pltpu.SMEM)] + [vmem] * 2,
        out_specs=(vmem,) * 5,
        scratch_shapes=[
            pltpu.VMEM((count, count, width, width), f32),
            pltpu.VMEM((count, count, width, width), f32),
            pltpu.VMEM((count, count, width, width), f32),
            pltpu.VMEM((count, count, width, width), f32),
            pltpu.VMEM((count, count, width, width), f32),
            pltpu.VMEM((SUB, LANES), f32),
            pltpu.VMEM((SUB, LANES), f32),
        ] + [sq] * 8 + [pltpu.VMEM((count, 1, width), f32), pltpu.VMEM((count, width, 1), f32), pltpu.VMEM((1, width), f32)],
        compiler_params=pltpu.CompilerParams(vmem_limit_bytes=32 * 1024 * 1024),
    )(place, f, h)


MESH_ID = pl.DeviceIdType.MESH
CHUNKS = 4


def sums_kernel(a_ref, f_ref, h_ref, r_ref, s_ref, in1, in2, acc, es, er, hs, hr, ds, dr):
    width, rows = a_ref.shape
    half = rows // 2
    step = half // CHUNKS
    total = 2 * width
    mat, q, row = lax.axis_index('mat'), lax.axis_index('col'), lax.axis_index('row')
    core = row % 2
    core_peer = (mat, q, row + 1 - 2 * core)
    x_peer = (mat, q, (row + 2) % 4)
    y_peer = (mat, 1 - q, row)

    def copy(src, dst, send, recv, peer):
        return pltpu.make_async_remote_copy(src_ref=src, dst_ref=dst, send_sem=send, recv_sem=recv, device_id=peer, device_id_type=MESH_ID)

    barrier = pltpu.get_barrier_semaphore()
    for peer in (core_peer, x_peer, y_peer):
        pl.semaphore_signal(barrier, inc=1, device_id=peer, device_id_type=MESH_ID)
    pl.semaphore_wait(barrier, 3)

    swaps = []
    for c in range(CHUNKS):
        src = a_ref.at[:, pl.ds(pl.multiple_of((1 - q) * half + c * step, step), step)]
        swaps.append(copy(src, r_ref.at[:, pl.ds(c * step, step)], es.at[c], er.at[c], y_peer))
        swaps[-1].start()
    top = a_ref.at[:, pl.ds(0, total)]
    h_y = copy(top, h_ref.at[q], hs.at[0], hr.at[1], y_peer)
    h_x0 = copy(top, h_ref.at[q], hs.at[1], hr.at[0], x_peer)
    h_c0 = copy(top, h_ref.at[q], hs.at[2], hr.at[0], core_peer)
    h_x1 = copy(h_ref.at[1 - q], h_ref.at[1 - q], hs.at[3], hr.at[1], x_peer)
    h_c1 = copy(h_ref.at[1 - q], h_ref.at[1 - q], hs.at[4], hr.at[1], core_peer)
    f_c0 = copy(h_ref.at[q], h_ref.at[q], hs.at[2], hr.at[0], core_peer)

    @pl.when(row == 0)
    def _():
        h_x0.start()
        h_c0.start()
        h_ref[q] = a_ref[:, 0:total]

    s_ref[...] = jnp.zeros_like(s_ref)

    def own(i, carry):
        tile = a_ref[:, pl.ds(pl.multiple_of(i * 256, 256), 256)]
        s_ref[0:width] += dot(tile, tile, 1, 1)
        return carry

    lax.fori_loop(0, rows // 256, own, 0)

    @pl.when(row == 2)
    def _():
        h_x0.wait_recv()
        f_c0.start()

    own_c = copy(s_ref.at[pl.ds(0, width)], in1, ds.at[0], dr.at[0], core_peer)
    own_x = copy(acc.at[0], in2.at[0], ds.at[1], dr.at[1], x_peer)
    own_y = copy(f_ref.at[q], f_ref.at[q], ds.at[2], dr.at[2], y_peer)
    own_b = copy(f_ref.at[q], f_ref.at[q], ds.at[3], dr.at[3], core_peer)
    own_o = copy(f_ref.at[1 - q], f_ref.at[1 - q], ds.at[4], dr.at[4], core_peer)

    @pl.when(core == 1)
    def _():
        own_c.start()

    @pl.when(core == 0)
    def _():
        own_c.wait_recv()
        acc[0] = s_ref[0:width] + in1[...]
        own_x.start()
        own_x.wait()
        f_ref[q] = acc[0] + in2[0]
        own_y.start()
        own_b.start()

    @pl.when(row == 0)
    def _():
        h_y.start()

    first = q == 0
    for c in range(CHUNKS):
        swaps[c].wait_recv()
        mine = a_ref[:, pl.ds(pl.multiple_of(q * half + c * step, step), step)]
        other = r_ref[:, c * step:(c + 1) * step]
        s_ref[width:] += dot(jnp.where(first, mine, other), jnp.where(first, other, mine), 1, 1)

    x_c = copy(s_ref.at[pl.ds(width, width)], in1, ds.at[0], dr.at[0], core_peer)
    x_y = copy(acc.at[0], in2.at[0], ds.at[1], dr.at[1], y_peer)
    x_x = copy(acc.at[1], in2.at[1], ds.at[2], dr.at[2], x_peer)
    x_b = copy(f_ref.at[2], f_ref.at[2], ds.at[5], dr.at[5], core_peer)

    @pl.when(core == 0)
    def _():
        x_c.start()

    @pl.when(core == 1)
    def _():
        own_c.wait_send()
        x_c.wait_recv()
        acc[0] = s_ref[width:] + in1[...]
        x_y.start()
        x_y.wait()
        acc[1] = acc[0] + in2[0]
        x_x.start()
        x_x.wait()
        f_ref[2] = acc[1] + in2[1]
        x_b.start()
        x_b.wait_send()
        own_b.wait_recv()
        own_o.wait_recv()

    @pl.when(core == 0)
    def _():
        own_y.wait()
        own_o.start()
        own_b.wait_send()
        x_c.wait_send()

    @pl.when(row == 0)
    def _():
        h_y.wait()
        h_x1.start()
        h_c1.start()
        h_x0.wait_send()
        h_c0.wait_send()
        h_x1.wait_send()
        h_c1.wait_send()

    @pl.when(row == 2)
    def _():
        h_x1.wait_recv()
        h_c1.start()
        f_c0.wait_send()
        h_c1.wait_send()

    @pl.when(core == 1)
    def _():
        h_c0.wait_recv()
        h_c1.wait_recv()

    @pl.when(core == 0)
    def _():
        own_o.wait_send()
        x_b.wait_recv()

    for c in range(CHUNKS):
        swaps[c].wait_send()


def sums_call(a2):
    width, rows = a2.shape
    f32 = jnp.float32
    vmem = pl.BlockSpec(memory_space=pltpu.VMEM)
    dma = pltpu.SemaphoreType.DMA
    return pl.pallas_call(
        sums_kernel,
        out_shape=(jax.ShapeDtypeStruct((3, width, width), f32), jax.ShapeDtypeStruct((2, width, 2 * width), f32), jax.ShapeDtypeStruct((width, rows // 2), f32)),
        in_specs=[vmem],
        out_specs=(vmem,) * 3,
        scratch_shapes=[
            pltpu.VMEM((2 * width, width), f32),
            pltpu.VMEM((width, width), f32),
            pltpu.VMEM((2, width, width), f32),
            pltpu.VMEM((2, width, width), f32),
            dma((CHUNKS,)), dma((CHUNKS,)), dma((5,)), dma((2,)), dma((6,)), dma((6,)),
        ],
        compiler_params=pltpu.CompilerParams(collective_id=0, has_side_effects=True, vmem_limit_bytes=20 * 1024 * 1024),
    )(a2)


def v_kernel(place, a_ref, near_ref, far_ref, xi_ref, top_ref, out_ref, x0_ref, x1_ref):
    slots, count, width, _ = xi_ref.shape
    half = near_ref.shape[1]
    q, row = place[0], place[1]
    x0_ref[...] = jnp.concatenate([xi_ref[0, i].T for i in range(2)], axis=1)
    x1_ref[...] = jnp.concatenate([xi_ref[1, i].T for i in range(count)], axis=1)

    def rows_of(far, base, c):
        at = pl.multiple_of(base + c * 256, 256)
        own = a_ref[:, pl.ds(at, 256)]
        par = far[:, pl.ds(pl.multiple_of(c * 256, 256), 256)]
        both = jnp.concatenate([own[:width], par[:width], own[width:], par[width:]], axis=0)
        out_ref[:width, pl.ds(at, 256)] = dot(x0_ref[...], both[:2 * width])
        out_ref[width:, pl.ds(at, 256)] = dot(x1_ref[...], both)

    def step(c, carry):
        rows_of(near_ref, q * half, c)
        rows_of(far_ref, (1 - q) * half, c)
        return carry

    lax.fori_loop(0, half // 256, step, 0)

    @pl.when(row == 0)
    def _():
        for s in range(slots):
            out_ref[s * width:(s + 1) * width, 0:count * width] = jnp.concatenate([top_ref[s, i].T for i in range(count)], axis=1)


def v_call(place, a2, near, far, xi, top):
    f32 = jnp.float32
    width = xi.shape[-1]
    vmem = pl.BlockSpec(memory_space=pltpu.VMEM)
    return pl.pallas_call(
        v_kernel,
        out_shape=jax.ShapeDtypeStruct(a2.shape, f32),
        in_specs=[pl.BlockSpec(memory_space=pltpu.SMEM)] + [vmem] * 5,
        out_specs=vmem,
        scratch_shapes=[pltpu.VMEM((width, 2 * width), f32), pltpu.VMEM((width, 4 * width), f32)],
        compiler_params=pltpu.CompilerParams(vmem_limit_bytes=24 * 1024 * 1024),
    )(place, a2, near, far, xi, top)


def col_sum(x):
    return x + lax.ppermute(x, 'col', [(0, 1), (1, 0)])


def row_sum(x):
    x = x + lax.ppermute(x, 'row', [(i, i ^ 1) for i in range(4)])
    return x + lax.ppermute(x, 'row', [(i, i ^ 2) for i in range(4)])


def factor_panel(panel, row_start, diag_start):
    loc_rows, width = panel.shape
    row_ids = row_start + jnp.arange(loc_rows)[:, None]
    col_ids = jnp.arange(width)

    def col_step(col_k, carry):
        panel_now, tau_vec = carry
        diag_row = diag_start + col_k
        col_x = lax.dynamic_slice_in_dim(panel_now, col_k, 1, axis=1)
        is_below = row_ids > diag_row
        at_diag = row_ids == diag_row
        x_below = jnp.where(is_below, col_x, 0.0)
        pick_rows = jnp.concatenate([at_diag.astype(jnp.float32), x_below], axis=1)
        red_pair = jnp.einsum('rt,rc->tc', pick_rows, panel_now, precision=FULL_PREC, preferred_element_type=jnp.float32)
        red_pair = row_sum(red_pair)
        row_k = red_pair[0]
        dot_vals = red_pair[1]
        alpha_val = jnp.sum(jnp.where(col_ids == col_k, row_k, 0.0))
        norm_val = jnp.sqrt(alpha_val * alpha_val + jnp.sum(jnp.where(col_ids == col_k, dot_vals, 0.0)))
        beta_val = jnp.where(alpha_val >= 0.0, -norm_val, norm_val)
        tau_k = (beta_val - alpha_val) / beta_val
        scale_k = 1.0 / (alpha_val - beta_val)
        w_row = jnp.where(col_ids > col_k, row_k + scale_k * dot_vals, 0.0)
        v_col = jnp.where(is_below, col_x * scale_k, at_diag.astype(jnp.float32))
        panel_now = panel_now - (tau_k * v_col) * w_row[None, :]
        new_col = jnp.where(is_below, col_x * scale_k, jnp.where(at_diag, beta_val, col_x))
        panel_now = lax.dynamic_update_slice_in_dim(panel_now, new_col, col_k, axis=1)
        tau_vec = jnp.where(col_ids == col_k, tau_k, tau_vec)
        return panel_now, tau_vec

    return lax.fori_loop(0, width, col_step, (panel, jnp.zeros((width,), jnp.float32)))


def build_t(v_gram, tau_vec):
    width = tau_vec.shape[0]
    col_ids = jnp.arange(width)

    def col_step(col_i, t_mat):
        g_col = lax.dynamic_slice_in_dim(v_gram, col_i, 1, axis=1)[:, 0]
        g_col = jnp.where(col_ids < col_i, g_col, 0.0)
        tau_i = jnp.sum(jnp.where(col_ids == col_i, tau_vec, 0.0))
        t_col = -tau_i * jnp.dot(t_mat, g_col, precision=FULL_PREC, preferred_element_type=jnp.float32)
        t_col = jnp.where(col_ids == col_i, tau_i, t_col)
        return jnp.where(col_ids[None, :] == col_i, t_col[:, None], t_mat)

    return lax.fori_loop(0, width, col_step, jnp.zeros((width, width), jnp.float32))


def column_plan(a_blk, col_count):
    loc_rows, loc_panels, width = a_blk.shape
    me_col = lax.axis_index('col')
    row_start = lax.axis_index('row') * loc_rows
    row_ids = row_start + jnp.arange(loc_rows)[:, None]
    col_ids = jnp.arange(width)[None, :]
    slots = jnp.arange(loc_panels)

    def step(panel_j, carry):
        work, tau_all, t_all = carry
        own_col = panel_j % col_count
        slot = panel_j // col_count
        is_owner = me_col == own_col
        head = lax.dynamic_slice_in_dim(work, slot, 1, axis=1)[:, 0]
        fac, tau_vec = factor_panel(head, row_start, panel_j * width)
        diag_cols = panel_j * width + col_ids
        v_mat = jnp.where(row_ids > diag_cols, fac, (row_ids == diag_cols).astype(jnp.float32))
        v_gram = row_sum(jnp.einsum('rk,rl->kl', v_mat, v_mat, precision=FULL_PREC, preferred_element_type=jnp.float32))
        t_mat = build_t(v_gram, tau_vec)
        packed = col_sum(jnp.where(is_owner, jnp.concatenate([v_mat, t_mat], axis=0), 0.0))
        v_own, t_own = packed[:loc_rows], packed[loc_rows:]
        w_sum = row_sum(jnp.einsum('rk,rsc->ksc', v_own, work, precision=FULL_PREC, preferred_element_type=jnp.float32))
        w_mat = jnp.einsum('kl,ksc->lsc', t_own, w_sum, precision=FULL_PREC, preferred_element_type=jnp.float32)
        later = slots * col_count + me_col > panel_j
        w_mat = jnp.where(later[None, :, None], w_mat, 0.0)
        new = work - jnp.einsum('rl,lsc->rsc', v_own, w_mat, precision=FULL_PREC, preferred_element_type=jnp.float32)
        mine = is_owner & (slots == slot)
        work = jnp.where(mine[None, :, None], fac[:, None, :], jnp.where(later[None, :, None], new, work))
        tau_all = jnp.where(mine[:, None], tau_vec[None], tau_all)
        t_all = jnp.where(mine[:, None, None], t_mat[None], t_all)
        return work, tau_all, t_all

    init = (a_blk, jnp.zeros((loc_panels, width), jnp.float32), jnp.zeros((loc_panels, width, width), jnp.float32))
    return lax.fori_loop(0, loc_panels * col_count, step, init)


def solution(mesh):
    col_count = mesh.shape['col']
    spec_a = P(('mat', 'row'), 'col', None)
    spec_tau = P(('mat', 'col'), None)
    spec_t = P(('mat', 'col'), None, None)

    def per_device(a_blk):
        loc_rows, loc_panels, width = a_blk.shape
        count = loc_panels * col_count
        me_col = lax.axis_index('col')
        me_row = lax.axis_index('row')
        half = loc_rows // 2
        place = jnp.stack([me_col, me_row]).astype(jnp.int32)
        a2 = a_blk.transpose(1, 2, 0).reshape(loc_panels * width, loc_rows)
        f, h, near = sums_call(a2)
        a_tied, f = lax.optimization_barrier((a2, f))
        far = lax.ppermute(lax.dynamic_slice_in_dim(a_tied, me_col * half, half, axis=1), 'col', [(0, 1), (1, 0)])
        top, x_inv, t_mat, tau, bad = factor_call(place, f, h, count, width)

        def gram_plan():
            v_all = v_call(place, a2, near, far, x_inv, top)
            return v_all.reshape(loc_panels, width, loc_rows).transpose(2, 0, 1), tau[:, 0], t_mat

        def safe_plan():
            return column_plan(a_blk * jnp.minimum(bad[0, 0], 1.0), col_count)

        return lax.cond(bad[0, 0] < 0.5, gram_plan, safe_plan)

    return jax.shard_map(per_device, mesh=mesh, in_specs=(spec_a,), out_specs=(spec_a, spec_tau, spec_t), check_vma=False)
```

profile of v0, /device:TPU:0, one launch (start us, length us, event | category | flops | bytes accessed | tf_op | source)
XLA Modules:
  0.0 186.4 jit_solution(4982001664394200347)
XLA Ops:
  0.6 81.2 %shard_map.38 = (f32[3,384,384]{2,1,0:T(8,128)S(1)}, f32[2,384,768]{2,1,0:T(8,128)S(1)}, f32[384,1024]{1,0:T(8,128)}) custom-call(f32[384,2048]{1,0:T(8,128)} %bitcast.87), custom_call_target="tpu_custom_call" | custom-call | tf_op jit(solution)/shard_map/pallas_call | solution.py:403
  81.9 0.0 copy-start
  81.9 1.2 copy-done
  83.1 2.8 %constant_dynamic-slice_fusion.2 = f32[384,1024]{1,0:T(8,128)} fusion(f32[384,2048]{1,0:T(8,128)} %bitcast.88, s32[]{:T(128)S(6)} %select_n.243), kind=kLoop, calls=%fused_computation.63 | loop fusion | bytes 3145732 | tf_op jit(solution)/shard_map/dynamic_slice | solution.py:570
  85.8 0.5 collective-permute-start.7
  86.4 0.1 pad_add_fusion.place
  86.5 0.0 copy-start.1
  86.5 1.5 copy-done.1
  87.9 82.1 %shard_map.39 = (f32[2,4,192,192]{3,2,1,0:T(8,128)}, f32[2,4,192,192]{3,2,1,0:T(8,128)}, f32[2,192,192]{2,1,0:T(8,128)}, f32[2,1,192]{2,1,0:T(1,128)}, f32[8,128]{1,0:T(8,128)S(1)}) custom-call(s32[2]{0:T(128)S(1)} %pad_add_fusion.place, f32[3,384,384]{2,1,0:T(8,128)S(1)} %copy-done.1, f32[2,384,768]{2,1,0:T(8,128)S(1)} %get-tuple-element.513.h_in), custom_call_target="tpu_custom_call" | custom-call | tf_op jit(solution)/shard_map/pallas_call | solution.py:230
  170.1 0.5 slice.40
  171.2 0.0 collective-permute-done.7
  171.3 15.1 %conditional.1 = (f32[2048,2,192]{0,2,1:T(8,128)}, f32[2,192]{1,0:T(2,128)}, f32[2,192,192]{2,1,0:T(8,128)}) conditional(s32[]{:T(128)} %bitcast.8, (f32[8,128]{1,0:T(8,128)S(1)}, f32[2048,2,192]{0,2,1:T(8,128)}) %tuple.71, (s32[2]{0:T(128)S(1)}, f32[384,2048]{1,0:T(8,128)}, f32[384,1024]{1,0:T(8,128)}, f32[384,1024]{1,0:T(8,128)}, ...), branch_computations={%region_0.10_spmd, %region_10.11_spmd} | conditional | flops 4716988416 | bytes 63960072 | solution.py:580
  171.5 0.0 copy-start.3
  171.5 14.3 %branch_1_fun.1 = f32[384,2048]{1,0:T(8,128)} custom-call(s32[2]{0:T(128)S(1)} %get-tuple-element.490.place, f32[384,2048]{1,0:T(8,128)} %get-tuple-element.491.a_ref, f32[384,1024]{1,0:T(8,128)} %get-tuple-element.492.near_ref, f32[384,1024]{1,0:T(8,128)} %get-tuple-element.493.far_ref, f32[2,4,192,192]{3,2,1,0:T(8,128)} %get-tuple-element.494.xi_ref, ...), custom_call_target="tpu_custom_call" | custom-call | tf_op jit(solution)/shard_map/cond/branch_1_fun/pallas_call | solution.py:451
  185.8 0.0 copy-done.3
  185.8 0.6 copy.12
Async XLA Ops:
  81.9 1.2 copy-start
  85.8 85.4 %collective-permute-start.7 = (f32[384,1024]{1,0:T(8,128)}, f32[384,1024]{1,0:T(8,128)}, u32[]{:S(2)}, u32[]{:S(2)}) collective-permute-start(f32[384,1024]{1,0:T(8,128)} %constant_dynamic-slice_fusion.2), channel_id=1, source_target_pairs={{0,4},{4,0},{1,5},{5,1},{2,6},{6,2},{3,7},{7,3}} | collective-permute-start | bytes 4718600 | tf_op jit(solution)/shard_map/ppermute | solution.py:570
  86.5 1.5 copy-start.1
  171.5 14.3 %copy-start.3 = (f32[2,1,192]{2,1,0:T(1,128)S(1)}, f32[2,1,192]{2,1,0:T(1,128)}, u32[]{:S(2)}) copy-start(f32[2,1,192]{2,1,0:T(1,128)} %get-tuple-element.496) | copy-start | bytes 4612 | tf_op jit(solution)/shard_map/cond
where the time goes:
time: 188 us; the launch traced here: 186 us
  Pallas kernels  178 us (95%)
  local copies, waits for them, and re-layouts  6.52 us (3%)
    pallas_call x1, Pallas kernels, factor_call(): pl.pallas_call(functools.partial(factor_kernel, count, width), out_shape=...  82.1 us
    pallas_call x1, Pallas kernels, sums_call(): pl.pallas_call(sums_kernel, out_shape=(jax.ShapeDtypeStruct((3, width, wi...  81.2 us
    pallas_call x1, Pallas kernels, v_call(): pl.pallas_call(v_kernel, out_shape=jax.ShapeDtypeStruct(a2.shape, f32), i...  14.3 us
  transfers between devices with their start and end apart: 1, of which 0 were waited for; matrix products, arithmetic and copies ran while one was open for 0% of the time, Pallas kernels for 44%

commit v1 on v0

--- a/solution.py
+++ b/solution.py
@@ -25,50 +25,51 @@
     eye = (lax.broadcasted_iota(jnp.int32, (n, n), 0) == lax.broadcasted_iota(jnp.int32, (n, n), 1)).astype(jnp.float32)
     gp = jnp.concatenate([g, zero], axis=1)
     bp = jnp.concatenate([b, eye], axis=1)
-    gt = [gp[8 * i:8 * i + 8] for i in range(nt)]
-    bt = [bp[8 * i:8 * i + 8] for i in range(nt)]
     lane = lax.broadcasted_iota(jnp.int32, (8, LANES), 1)
     row8 = lax.broadcasted_iota(jnp.int32, (8, LANES), 0)
-    lane1 = lane[0:1]
-    tau_row = jnp.zeros((1, LANES), jnp.float32)
-    piv_row = jnp.zeros((1, LANES), jnp.float32)
-    sgn_row = jnp.zeros((1, LANES), jnp.float32)
     full = (8, LANES)
 
     def row_of(tile, r):
         return jnp.broadcast_to(tile[r:r + 1, :], full)
 
-    for q in range(nt):
-        eg = [[jnp.broadcast_to(gt[i][:, 8 * q + c:8 * q + c + 1], full) for c in range(8)] for i in range(nt)]
-        eb = [[jnp.broadcast_to(bt[i][:, 8 * q + c:8 * q + c + 1], full) for c in range(8)] for i in range(nt)]
+    def group(q, carry):
+        gt, bt, rows = list(carry[0]), list(carry[1]), list(carry[2])
+        base = 8 * q
+        picks = [lane == base + c for c in range(8)]
+
+        def spread(tile):
+            return [jnp.broadcast_to(jnp.sum(jnp.where(picks[c], tile, 0.0), axis=1, keepdims=True), full) for c in range(8)]
+
+        eg = [spread(t) for t in gt]
+        eb = [spread(t) for t in bt]
+        r_tile = jnp.zeros(full, jnp.float32)
+        x_tile = jnp.zeros(full, jnp.float32)
         for r in range(8):
-            k = 8 * q + r
             at_row = row8 == r
-            right = lane > k
-            here = lane == k
-            piv = row_of(eg[q][r], r)
+            right = lane > base + r
+            here = picks[r]
+            piv = row_of(eg[0][r], r)
             inv = 1.0 / piv
             root = jnp.sqrt(piv)
             unit = root * inv
-            g_cols = [row_of(eg[q][c], r) for c in range(r + 1, 8)]
-            row_g = row_of(gt[q], r)
-            g_right = jnp.where(right, row_g, 0.0)
+            g_cols = [row_of(eg[0][c], r) for c in range(r + 1, 8)]
+            g_right = jnp.where(right, row_of(gt[0], r), 0.0)
             g_keep = jnp.where(here, inv, g_right)
-            alpha = row_of(eb[q][r], r)
+            alpha = row_of(eb[0][r], r)
             s = jnp.where(alpha >= 0.0, 1.0, -1.0)
             beta = -s * root
             xkk = alpha - beta
             rx = 1.0 / xkk
             su = s * unit
-            x_cols = [row_of(eb[q][c], r) + su * g_cols[c - r - 1] for c in range(r + 1, 8)]
-            row_b = row_of(bt[q], r)
+            x_cols = [row_of(eb[0][c], r) + su * g_cols[c - r - 1] for c in range(r + 1, 8)]
+            row_b = row_of(bt[0], r)
             r_row = -(su * g_right)
             x_right = jnp.where(right, row_b - r_row, 0.0)
             x_keep = jnp.where(here, rx, jnp.where(right, x_right, row_b))
             for i in range(nt):
                 m = eg[i][r] * inv
                 wide = jnp.where(here, m, gt[i] - m * g_right)
-                if i == q:
+                if i == 0:
                     wide = jnp.where(at_row, g_keep, wide)
                     m = jnp.where(at_row, 0.0, m)
                 gt[i] = wide
@@ -77,20 +78,27 @@
             for i in range(nt):
                 m = eb[i][r] * rx
                 wide = jnp.where(here, m, bt[i] - m * x_right)
-                if i == q:
+                if i == 0:
                     wide = jnp.where(at_row, x_keep, wide)
                 bt[i] = wide
                 for c in range(r + 1, 8):
                     new = eb[i][c] - m * x_cols[c - r - 1]
-                    if i == q:
+                    if i == 0:
                         new = jnp.where(at_row, x_cols[c - r - 1], new)
                     eb[i][c] = new
-            r_ref[k:k + 1, :] = jnp.where(here, beta, r_row)[0:1]
-            x_ref[k:k + 1, :] = jnp.where(here, xkk, x_right)[0:1]
-            here1 = lane1 == k
-            tau_row = jnp.where(here1, ((beta - alpha) / beta)[0:1], tau_row)
-            piv_row = jnp.where(here1, piv[0:1], piv_row)
-            sgn_row = jnp.where(here1, beta[0:1], sgn_row)
+            r_tile = jnp.where(at_row, jnp.where(here, beta, r_row), r_tile)
+            x_tile = jnp.where(at_row, jnp.where(here, xkk, x_right), x_tile)
+            for j, val in enumerate(((beta - alpha) / beta, piv, beta)):
+                rows[j] = jnp.where(here, val, rows[j])
+        at = pl.multiple_of(base, 8)
+        r_ref[pl.ds(at, 8), :] = r_tile
+        x_ref[pl.ds(at, 8), :] = x_tile
+        return tuple(gt[1:] + gt[:1]), tuple(bt[1:] + bt[:1]), tuple(rows)
+
+    blank = jnp.zeros(full, jnp.float32)
+    init = tuple(gp[8 * i:8 * i + 8] for i in range(nt)), tuple(bp[8 * i:8 * i + 8] for i in range(nt)), (blank,) * 3
+    gt, bt, (tau_t, piv_t, sgn_t) = lax.fori_loop(0, nt, group, init)
+    tau_row, piv_row, sgn_row = tau_t[0:1], piv_t[0:1], sgn_t[0:1]
     mg = jnp.concatenate(gt, axis=0)[:, :n]
     mb = jnp.concatenate(bt, axis=0)[:, :n]
     ri = lax.broadcasted_iota(jnp.int32, (n, n), 0)
@@ -104,7 +112,7 @@
     return v, x_inv, r_inv, tau_row[:, :n], piv_row[:, :n]
 
 
-def factor_kernel(count, width, place, f_in, h_in, top_out, xi_out, t_ref, tau_ref, ok_ref, top_ref, xi_ref, g_ref, w_ref, x_ref, rb_ref, xb_ref, gs, bs, ri_s, vi_s, xi_s, rs, xs, vs, dg_ref, dc_ref, tau_s):
+def factor_kernel(count, width, q, f_in, h_in, top_out, xi_out, t_ref, tau_ref, ok_ref, top_ref, xi_ref, g_ref, w_ref, x_ref, rb_ref, xb_ref, gs, bs, ri_s, vi_s, xi_s, rs, xs, vs, dg_ref, dc_ref, tau_s):
     subs = width // SUB
     ri = lax.broadcasted_iota(jnp.int32, (width, width), 0)
     ci = lax.broadcasted_iota(jnp.int32, (width, width), 1)
@@ -122,7 +130,6 @@
                     g_ref[i, j] = f_in[2, sj:sj + width, si:si + width].T
         dg_ref[i] = jnp.sum(jnp.where(ri == ci, g_ref[i, i], 0.0), axis=0, keepdims=True)
         dc_ref[i] = jnp.sqrt(jnp.sum(jnp.where(ri == ci, g_ref[i, i], 0.0), axis=1, keepdims=True))
-    q = place[0]
     xi_out[...] = jnp.zeros_like(xi_out)
 
     def panel(j, bad):
@@ -222,34 +229,11 @@
     ok_ref[...] = jnp.full(ok_ref.shape, bad, jnp.float32)
 
 
-def factor_call(place, f, h, count, width):
-    f32 = jnp.float32
-    blocks = jax.ShapeDtypeStruct((2, count, width, width), f32)
-    vmem = pl.BlockSpec(memory_space=pltpu.VMEM)
-    sq = pltpu.VMEM((width, width), f32)
-    return pl.pallas_call(
-        functools.partial(factor_kernel, count, width),
-        out_shape=(blocks, blocks, jax.ShapeDtypeStruct((2, width, width), f32), jax.ShapeDtypeStruct((2, 1, width), f32), jax.ShapeDtypeStruct((8, 128), f32)),
-        in_specs=[pl.BlockSpec(memory_space=pltpu.SMEM)] + [vmem] * 2,
-        out_specs=(vmem,) * 5,
-        scratch_shapes=[
-            pltpu.VMEM((count, count, width, width), f32),
-            pltpu.VMEM((count, count, width, width), f32),
-            pltpu.VMEM((count, count, width, width), f32),
-            pltpu.VMEM((count, count, width, width), f32),
-            pltpu.VMEM((count, count, width, width), f32),
-            pltpu.VMEM((SUB, LANES), f32),
-            pltpu.VMEM((SUB, LANES), f32),
-        ] + [sq] * 8 + [pltpu.VMEM((count, 1, width), f32), pltpu.VMEM((count, width, 1), f32), pltpu.VMEM((1, width), f32)],
-        compiler_params=pltpu.CompilerParams(vmem_limit_bytes=32 * 1024 * 1024),
-    )(place, f, h)
-
-
 MESH_ID = pl.DeviceIdType.MESH
 CHUNKS = 4
 
 
-def sums_kernel(a_ref, f_ref, h_ref, r_ref, s_ref, in1, in2, acc, es, er, hs, hr, ds, dr):
+def sums_kernel(a_ref, r_ref, f_ref, h_ref, s_ref, in1, in2, acc, es, er, hs, hr, ds, dr):
     width, rows = a_ref.shape
     half = rows // 2
     step = half // CHUNKS
@@ -395,24 +379,37 @@
         swaps[c].wait_send()
 
 
-def sums_call(a2):
-    width, rows = a2.shape
+def joint_kernel(count, width, a_ref, top_out, xi_out, t_ref, tau_ref, ok_ref, r_ref, *rest):
+    sums, sems, scratch = rest[:6], rest[6:12], rest[12:]
+    sums_kernel(a_ref, r_ref, *sums, *sems)
+    factor_kernel(count, width, lax.axis_index('col'), sums[0], sums[1], top_out, xi_out, t_ref, tau_ref, ok_ref, *scratch)
+
+
+def joint_call(a2, count, width):
+    cols, rows = a2.shape
     f32 = jnp.float32
     vmem = pl.BlockSpec(memory_space=pltpu.VMEM)
     dma = pltpu.SemaphoreType.DMA
+    grid = pltpu.VMEM((count, count, width, width), f32)
+    sq = pltpu.VMEM((width, width), f32)
+    blocks = jax.ShapeDtypeStruct((2, count, width, width), f32)
     return pl.pallas_call(
-        sums_kernel,
-        out_shape=(jax.ShapeDtypeStruct((3, width, width), f32), jax.ShapeDtypeStruct((2, width, 2 * width), f32), jax.ShapeDtypeStruct((width, rows // 2), f32)),
+        functools.partial(joint_kernel, count, width),
+        out_shape=(blocks, blocks, jax.ShapeDtypeStruct((2, width, width), f32), jax.ShapeDtypeStruct((2, 1, width), f32), jax.ShapeDtypeStruct((8, 128), f32), jax.ShapeDtypeStruct((cols, rows // 2), f32)),
         in_specs=[vmem],
-        out_specs=(vmem,) * 3,
+        out_specs=(vmem,) * 6,
         scratch_shapes=[
-            pltpu.VMEM((2 * width, width), f32),
-            pltpu.VMEM((width, width), f32),
-            pltpu.VMEM((2, width, width), f32),
-            pltpu.VMEM((2, width, width), f32),
+            pltpu.VMEM((3, cols, cols), f32),
+            pltpu.VMEM((2, cols, 2 * cols), f32),
+            pltpu.VMEM((2 * cols, cols), f32),
+            pltpu.VMEM((cols, cols), f32),
+            pltpu.VMEM((2, cols, cols), f32),
+            pltpu.VMEM((2, cols, cols), f32),
             dma((CHUNKS,)), dma((CHUNKS,)), dma((5,)), dma((2,)), dma((6,)), dma((6,)),
+        ] + [grid] * 5 + [pltpu.VMEM((SUB, LANES), f32)] * 2 + [sq] * 8 + [
+            pltpu.VMEM((count, 1, width), f32), pltpu.VMEM((count, width, 1), f32), pltpu.VMEM((1, width), f32),
         ],
-        compiler_params=pltpu.CompilerParams(collective_id=0, has_side_effects=True, vmem_limit_bytes=20 * 1024 * 1024),
+        compiler_params=pltpu.CompilerParams(collective_id=0, has_side_effects=True, vmem_limit_bytes=44 * 1024 * 1024),
     )(a2)
 
 
@@ -565,10 +562,8 @@
         half = loc_rows // 2
         place = jnp.stack([me_col, me_row]).astype(jnp.int32)
         a2 = a_blk.transpose(1, 2, 0).reshape(loc_panels * width, loc_rows)
-        f, h, near = sums_call(a2)
-        a_tied, f = lax.optimization_barrier((a2, f))
-        far = lax.ppermute(lax.dynamic_slice_in_dim(a_tied, me_col * half, half, axis=1), 'col', [(0, 1), (1, 0)])
-        top, x_inv, t_mat, tau, bad = factor_call(place, f, h, count, width)
+        far = lax.ppermute(lax.dynamic_slice_in_dim(a2, me_col * half, half, axis=1), 'col', [(0, 1), (1, 0)])
+        top, x_inv, t_mat, tau, bad, near = joint_call(a2, count, width)
 
         def gram_plan():
             v_all = v_call(place, a2, near, far, x_inv, top)

time: 188 us -> 206 us (1.096)
  Pallas kernels: 178 us -> 195 us
  starting transfers between devices: 0.54 us -> 3.39 us
  local copies, waits for them, and re-layouts: 6.52 us -> 3.96 us
    pallas_call x2 -> x1, Pallas kernels: 163 us -> 181 us  [joint_call(): pl.pallas_call(functools.partial(joint_kernel, count, width), out_shape=(...]
    ppermute x1, starting transfers between devices: 0.54 us -> 3.39 us  [per_device(): lax.ppermute(lax.dynamic_slice_in_dim(a2, me_col * half, half, axis=1), '...]
  transfers between devices with their start and end apart: 1 -> 1, of which waited for: 0 -> 0; matrix products, arithmetic and copies ran while one was open for 0% -> 1% of each run, Pallas kernels for 44% -> 89%
where the time goes in v1:
time: 206 us; the launch traced here: 204 us
  Pallas kernels  195 us (95%)
  local copies, waits for them, and re-layouts  3.96 us (2%)
  starting transfers between devices  3.39 us (2%)
    pallas_call x1, Pallas kernels, joint_call(): pl.pallas_call(functools.partial(joint_kernel, count, width), out_shape=(...  181 us
    pallas_call x1, Pallas kernels, v_call(): pl.pallas_call(v_kernel, out_shape=jax.ShapeDtypeStruct(a2.shape, f32), i...  13.8 us
  transfers between devices with their start and end apart: 1, of which 0 were waited for; matrix products, arithmetic and copies ran while one was open for 1% of the time, Pallas kernels for 89%

profile of v1, /device:TPU:0, one launch (start us, length us, event | category | flops | bytes accessed | tf_op | source)
XLA Modules:
  0.0 204.4 jit_solution(6259275364088696362)
XLA Ops:
  0.6 0.0 copy-start.3
  0.6 1.7 constant_dynamic-slice_fusion.2
  2.3 3.4 %collective-permute-start.7 = (f32[384,1024]{1,0:T(8,128)S(1)}, f32[384,1024]{1,0:T(8,128)S(1)}, u32[]{:S(2)}, u32[]{:S(2)}) collective-permute-start(f32[384,1024]{1,0:T(8,128)S(1)} %constant_dynamic-slice_fusion.2), channel_id=1, source_target_pairs={{0,4},{4,0},{1,5},{5,1},{2,6},{6,2},{3,7},{7,3}} | collective-permute-start | bytes 4718600 | tf_op jit(solution)/shard_map/ppermute | solution.py:565
  5.7 0.0 copy-done.3
  5.7 181.3 %shard_map.38 = (f32[2,4,192,192]{3,2,1,0:T(8,128)}, f32[2,4,192,192]{3,2,1,0:T(8,128)}, f32[2,192,192]{2,1,0:T(8,128)}, f32[2,1,192]{2,1,0:T(1,128)S(1)}, f32[8,128]{1,0:T(8,128)S(1)}, /*index=5*/f32[384,1024]{1,0:T(8,128)}) custom-call(f32[384,2048]{1,0:T(8,128)S(1)} %bitcast.90), custom_call_target="tpu_custom_call" | custom-call | tf_op jit(solution)/shard_map/pallas_call | solution.py:396
  187.0 0.5 slice.40
  188.2 0.6 pad_add_fusion
  188.9 0.0 collective-permute-done.7
  188.9 13.8 %conditional.1 = (f32[2048,2,192]{0,2,1:T(8,128)}, f32[2,192]{1,0:T(2,128)S(1)}, f32[2,192,192]{2,1,0:T(8,128)}) conditional(s32[]{:T(128)} %bitcast.5, (f32[8,128]{1,0:T(8,128)S(1)}, f32[2048,2,192]{0,2,1:T(8,128)}) %tuple.69, (s32[2]{0:T(128)}, f32[384,2048]{1,0:T(8,128)}, f32[384,1024]{1,0:T(8,128)}, f32[384,1024]{1,0:T(8,128)S(1)}, ...), branch_computations={%region_0.10_spmd, %region_10.11_spmd} | conditional | flops 4716988416 | bytes 102292544 | solution.py:575
  188.9 13.8 %branch_1_fun.1 = f32[384,2048]{1,0:T(8,128)} custom-call(s32[2]{0:T(128)} %get-tuple-element.490.place, f32[384,2048]{1,0:T(8,128)} %get-tuple-element.491.a_ref, f32[384,1024]{1,0:T(8,128)} %get-tuple-element.492.near_ref, f32[384,1024]{1,0:T(8,128)S(1)} %get-tuple-element.493.far_ref, f32[2,4,192,192]{3,2,1,0:T(8,128)} %get-tuple-element.494.xi_ref, ...), custom_call_target="tpu_custom_call" | custom-call | tf_op jit(solution)/shard_map/cond/branch_1_fun/pallas_call | solution.py:448
  202.7 0.0 copy-start.5
  202.7 1.8 copy.52
  204.4 0.0 copy-done.5
  (1 shorter events, 0.0 us)
Async XLA Ops:
  0.6 5.1 %copy-start.3 = (f32[2048,2,192]{0,2,1:T(8,128)S(1)}, f32[2048,2,192]{0,2,1:T(8,128)}, u32[]{:S(2)}) copy-start(f32[2048,2,192]{0,2,1:T(8,128)} %param.9) | copy-start | bytes 9437188
  2.3 186.5 %collective-permute-start.7 = (f32[384,1024]{1,0:T(8,128)S(1)}, f32[384,1024]{1,0:T(8,128)S(1)}, u32[]{:S(2)}, u32[]{:S(2)}) collective-permute-start(f32[384,1024]{1,0:T(8,128)S(1)} %constant_dynamic-slice_fusion.2), channel_id=1, source_target_pairs={{0,4},{4,0},{1,5},{5,1},{2,6},{6,2},{3,7},{7,3}} | collective-permute-start | bytes 4718600 | tf_op jit(solution)/shard_map/ppermute | solution.py:565
  202.7 1.8 copy-start.5

commit v2 on v1

--- a/solution.py
+++ b/solution.py
@@ -112,25 +112,250 @@
     return v, x_inv, r_inv, tau_row[:, :n], piv_row[:, :n]
 
 
-def factor_kernel(count, width, q, f_in, h_in, top_out, xi_out, t_ref, tau_ref, ok_ref, top_ref, xi_ref, g_ref, w_ref, x_ref, rb_ref, xb_ref, gs, bs, ri_s, vi_s, xi_s, rs, xs, vs, dg_ref, dc_ref, tau_s):
+MESH_ID = pl.DeviceIdType.MESH
+CHUNKS = 4
+TILE = 256
+
+
+def joint_kernel(count, width, a_ref, top_out, xi_out, t_ref, tau_ref, ok_ref, r_ref, f_ref, h_ref, s_ref, in1, in2, acc, p_ref, p_in, gd_ref, wp_ref,
+                 es, er, zs, zr, hs, hr, ds, dr, ps, pr, ws, wr,
+                 top_ref, xi_ref, g_ref, w_ref, x_ref, rb_ref, xb_ref, gs, bs, ri_s, vi_s, xi_s, rs, xs, vs, dg_ref, dc_ref, tau_s):
+    cols, rows = a_ref.shape
+    half = rows // 2
+    step = half // CHUNKS
+    total = 2 * cols
+    mat, q, row = lax.axis_index('mat'), lax.axis_index('col'), lax.axis_index('row')
+    core = row % 2
+    core_peer = (mat, q, row + 1 - 2 * core)
+    x_peer = (mat, q, (row + 2) % 4)
+    y_peer = (mat, 1 - q, row)
     subs = width // SUB
     ri = lax.broadcasted_iota(jnp.int32, (width, width), 0)
     ci = lax.broadcasted_iota(jnp.int32, (width, width), 1)
-    for i in range(count):
-        qi, si = i % 2, i // 2 * width
-        for j in range(count):
-            qj, sj = j % 2, j // 2 * width
-            w_ref[i, j] = h_in[qj, sj:sj + width, i * width:(i + 1) * width].T
-            if i <= j:
-                if qi == qj:
-                    g_ref[i, j] = f_in[qi, si:si + width, sj:sj + width]
-                elif qi == 0:
-                    g_ref[i, j] = f_in[2, si:si + width, sj:sj + width]
-                else:
-                    g_ref[i, j] = f_in[2, sj:sj + width, si:si + width].T
-        dg_ref[i] = jnp.sum(jnp.where(ri == ci, g_ref[i, i], 0.0), axis=0, keepdims=True)
-        dc_ref[i] = jnp.sqrt(jnp.sum(jnp.where(ri == ci, g_ref[i, i], 0.0), axis=1, keepdims=True))
+
+    def copy(src, dst, send, recv, peer):
+        return pltpu.make_async_remote_copy(src_ref=src, dst_ref=dst, send_sem=send, recv_sem=recv, device_id=peer, device_id_type=MESH_ID)
+
+    barrier = pltpu.get_barrier_semaphore()
+    for peer in (core_peer, x_peer, y_peer):
+        pl.semaphore_signal(barrier, inc=1, device_id=peer, device_id_type=MESH_ID)
+    pl.semaphore_wait(barrier, 3)
+
+    w_src = a_ref.at[pl.ds(0, width), pl.ds(0, TILE)]
+    w_y = copy(w_src, wp_ref, ws.at[0], wr.at[0], y_peer)
+    w_x0 = copy(w_src, wp_ref, ws.at[1], wr.at[0], x_peer)
+    w_c0 = copy(w_src, wp_ref, ws.at[2], wr.at[0], core_peer)
+    w_x1 = copy(wp_ref, wp_ref, ws.at[1], wr.at[0], x_peer)
+    w_c1 = copy(wp_ref, wp_ref, ws.at[2], wr.at[0], core_peer)
+    first_dev = jnp.logical_and(row == 0, q == 0)
+    relay_dev = jnp.logical_and(row == 0, q == 1)
+
+    @pl.when(first_dev)
+    def _():
+        w_y.start()
+        w_x0.start()
+        w_c0.start()
+        wp_ref[...] = a_ref[0:width, 0:TILE]
+
+    near, far = [], []
+    for c in range(CHUNKS):
+        at = pl.ds(pl.multiple_of((1 - q) * half + c * step, step), step)
+        near.append(copy(a_ref.at[:, at], r_ref.at[:, at], es.at[c], er.at[c], y_peer))
+        at = pl.ds(pl.multiple_of(q * half + c * step, step), step)
+        far.append(copy(a_ref.at[:, at], r_ref.at[:, at], zs.at[c], zr.at[c], y_peer))
+    near[0].start()
+
+    lo, hi = pl.ds(0, cols), pl.ds(cols, cols)
+    h_x0 = copy(a_ref.at[:, pl.ds(0, total)], h_ref.at[q], hs.at[0], hr.at[0], x_peer)
+    h_c0 = copy(a_ref.at[:, pl.ds(0, total)], h_ref.at[q], hs.at[1], hr.at[0], core_peer)
+    h_c2 = copy(h_ref.at[q], h_ref.at[q], hs.at[1], hr.at[0], core_peer)
+    h_ylo = copy(a_ref.at[:, lo], h_ref.at[q, :, lo], hs.at[2], hr.at[1], y_peer)
+    h_yhi = copy(h_ref.at[q, :, hi], h_ref.at[q, :, hi], hs.at[2], hr.at[2], y_peer)
+    h_xlo = copy(h_ref.at[1 - q, :, lo], h_ref.at[1 - q, :, lo], hs.at[3], hr.at[1], x_peer)
+    h_xhi = copy(h_ref.at[1 - q, :, hi], h_ref.at[1 - q, :, hi], hs.at[3], hr.at[2], x_peer)
+    h_clo = copy(h_ref.at[1 - q, :, lo], h_ref.at[1 - q, :, lo], hs.at[4], hr.at[1], core_peer)
+    h_chi = copy(h_ref.at[1 - q, :, hi], h_ref.at[1 - q, :, hi], hs.at[5], hr.at[2], core_peer)
+
+    p_ref[...] = jnp.zeros_like(p_ref)
+
+    def first_gram(i, carry):
+        tile = a_ref[0:width, pl.ds(pl.multiple_of(i * TILE, TILE), TILE)]
+        p_ref[...] += dot(tile, tile, 1, 1)
+        return carry
+
+    lax.fori_loop(0, rows // TILE, first_gram, 0)
+    p_c = copy(p_ref, p_in.at[0], ps.at[0], pr.at[0], core_peer)
+    p_x = copy(p_in.at[2], p_in.at[1], ps.at[1], pr.at[1], x_peer)
+    p_y = copy(gd_ref.at[q], gd_ref.at[q], ps.at[2], pr.at[2], y_peer)
+    p_c.start()
+
+    s_ref[...] = jnp.zeros_like(s_ref)
     xi_out[...] = jnp.zeros_like(xi_out)
+
+    def own(i, carry):
+        tile = a_ref[:, pl.ds(pl.multiple_of(i * TILE, TILE), TILE)]
+        s_ref[0:cols] += dot(tile, tile, 1, 1)
+        return carry
+
+    p_c.wait()
+    p_in[2] = p_ref[...] + p_in[0]
+    p_x.start()
+
+    @pl.when(row == 0)
+    def _():
+        h_x0.start()
+        h_c0.start()
+        h_ref[q] = a_ref[:, 0:total]
+
+    lax.fori_loop(0, rows // TILE // 2, own, 0)
+    p_x.wait()
+    gd_ref[q] = p_in[2] + p_in[1]
+    p_y.start()
+    for c in range(1, CHUNKS):
+        near[c].start()
+
+    @pl.when(relay_dev)
+    def _():
+        w_y.wait_recv()
+        w_x1.start()
+        w_c1.start()
+
+    @pl.when(row == 2)
+    def _():
+        w_x0.wait_recv()
+        w_c1.start()
+
+    lax.fori_loop(rows // TILE // 2, rows // TILE, own, 0)
+
+    own_c = copy(s_ref.at[pl.ds(0, cols)], in1, ds.at[0], dr.at[0], core_peer)
+    own_x = copy(acc.at[0], in2.at[0], ds.at[1], dr.at[1], x_peer)
+    own_y = copy(f_ref.at[q], f_ref.at[q], ds.at[2], dr.at[2], y_peer)
+    own_b = copy(f_ref.at[q], f_ref.at[q], ds.at[3], dr.at[3], core_peer)
+    own_o = copy(f_ref.at[1 - q], f_ref.at[1 - q], ds.at[4], dr.at[4], core_peer)
+    x_c = copy(s_ref.at[pl.ds(cols, cols)], in1, ds.at[0], dr.at[0], core_peer)
+    x_y = copy(acc.at[0], in2.at[0], ds.at[1], dr.at[1], y_peer)
+    x_x = copy(acc.at[1], in2.at[1], ds.at[2], dr.at[2], x_peer)
+    x_b = copy(f_ref.at[2], f_ref.at[2], ds.at[5], dr.at[5], core_peer)
+
+    @pl.when(row == 0)
+    def _():
+        h_ylo.start()
+
+    @pl.when(row == 2)
+    def _():
+        h_x0.wait_recv()
+        h_c2.start()
+        h_yhi.start()
+
+    @pl.when(core == 1)
+    def _():
+        own_c.start()
+        w_c0.wait_recv()
+
+    p_y.wait()
+    g_ref[0, 0] = gd_ref[0]
+    w_ref[0, 0] = wp_ref[:, 0:width].T
+
+    def diag_of(i, block):
+        dg_ref[i] = jnp.sum(jnp.where(ri == ci, block, 0.0), axis=0, keepdims=True)
+        dc_ref[i] = jnp.sqrt(jnp.sum(jnp.where(ri == ci, block, 0.0), axis=1, keepdims=True))
+
+    diag_of(0, gd_ref[0])
+
+    def own_stage1():
+        @pl.when(core == 0)
+        def _():
+            own_c.wait_recv()
+            acc[0] = s_ref[0:cols] + in1[...]
+            own_x.start()
+
+    def own_stage2():
+        @pl.when(core == 0)
+        def _():
+            own_x.wait()
+            f_ref[q] = acc[0] + in2[0]
+            own_y.start()
+            own_b.start()
+
+    def finish_sums():
+        first = q == 0
+        for c in range(CHUNKS):
+            near[c].wait_recv()
+            at = pl.ds(pl.multiple_of(q * half + c * step, step), step)
+            mine = a_ref[:, at]
+            other = r_ref[:, at]
+            s_ref[cols:] += dot(jnp.where(first, mine, other), jnp.where(first, other, mine), 1, 1)
+
+        @pl.when(core == 0)
+        def _():
+            x_c.start()
+
+        @pl.when(core == 1)
+        def _():
+            own_c.wait_send()
+            x_c.wait_recv()
+            acc[0] = s_ref[cols:] + in1[...]
+            x_y.start()
+            x_y.wait()
+            acc[1] = acc[0] + in2[0]
+            x_x.start()
+            x_x.wait()
+            f_ref[2] = acc[1] + in2[1]
+            x_b.start()
+
+        @pl.when(core == 0)
+        def _():
+            own_y.wait()
+            own_o.start()
+
+        @pl.when(row == 0)
+        def _():
+            h_ylo.wait()
+            h_xlo.start()
+            h_clo.start()
+            h_xhi.wait_recv()
+            h_chi.start()
+            h_x0.wait_send()
+            h_c0.wait_send()
+
+        @pl.when(row == 2)
+        def _():
+            h_yhi.wait()
+            h_xhi.start()
+            h_chi.start()
+            h_xlo.wait_recv()
+            h_clo.start()
+            h_c2.wait_send()
+
+        @pl.when(core == 0)
+        def _():
+            x_b.wait_recv()
+
+        @pl.when(core == 1)
+        def _():
+            h_c0.wait_recv()
+            h_clo.wait_recv()
+            h_chi.wait_recv()
+            own_b.wait_recv()
+            own_o.wait_recv()
+
+        for c in range(CHUNKS):
+            far[c].start()
+        for i in range(count):
+            qi, si = i % 2, i // 2 * width
+            for j in range(count):
+                qj, sj = j % 2, j // 2 * width
+                if i + j > 0:
+                    w_ref[i, j] = h_ref[qj, sj:sj + width, i * width:(i + 1) * width].T
+                    if i <= j:
+                        if qi == qj:
+                            g_ref[i, j] = f_ref[qi, si:si + width, sj:sj + width]
+                        elif qi == 0:
+                            g_ref[i, j] = f_ref[2, si:si + width, sj:sj + width]
+                        else:
+                            g_ref[i, j] = f_ref[2, sj:sj + width, si:si + width].T
+            if i > 0:
+                diag_of(i, g_ref[i, i])
 
     def panel(j, bad):
         gs[...] = g_ref[j, j]
@@ -142,6 +367,11 @@
             c0, c1 = s * SUB, (s + 1) * SUB
             v, x_inv, r_inv, tau, piv = factor_block(gs[c0:c1, c0:c1], bs[c0:c1, c0:c1], rb_ref, xb_ref)
             v_inv = xb_ref[:, SUB:2 * SUB]
+            if s < 2:
+                @pl.when(j == 0)
+                def _(stage=(own_stage1, own_stage2)[s]):
+                    stage()
+
             rs[c0:c1, c0:c1] = rb_ref[:, :SUB]
             xs[c0:c1, c0:c1] = xb_ref[:, :SUB]
             vs[c0:c1, c0:c1] = v
@@ -164,6 +394,11 @@
                 ri_s[:c0, c0:c1] = -dot(ri_s[:c0, :c0], dot(rs[:c0, c0:c1], r_inv))
                 vi_s[c0:c1, :c0] = -dot(dot(v_inv, vs[c0:c1, :c0]), vi_s[:c0, :c0])
         x_inv, r_inv, v_inv = xi_s[...], ri_s[...], vi_s[...]
+
+        @pl.when(j == 0)
+        def _():
+            finish_sums()
+
         xi_ref[j, j] = x_inv
         top_ref[j, j] = rs[...] + vs[...]
 
@@ -228,161 +463,44 @@
     bad = lax.fori_loop(0, count, panel, jnp.float32(0.0))
     ok_ref[...] = jnp.full(ok_ref.shape, bad, jnp.float32)
 
-
-MESH_ID = pl.DeviceIdType.MESH
-CHUNKS = 4
-
-
-def sums_kernel(a_ref, r_ref, f_ref, h_ref, s_ref, in1, in2, acc, es, er, hs, hr, ds, dr):
-    width, rows = a_ref.shape
-    half = rows // 2
-    step = half // CHUNKS
-    total = 2 * width
-    mat, q, row = lax.axis_index('mat'), lax.axis_index('col'), lax.axis_index('row')
-    core = row % 2
-    core_peer = (mat, q, row + 1 - 2 * core)
-    x_peer = (mat, q, (row + 2) % 4)
-    y_peer = (mat, 1 - q, row)
-
-    def copy(src, dst, send, recv, peer):
-        return pltpu.make_async_remote_copy(src_ref=src, dst_ref=dst, send_sem=send, recv_sem=recv, device_id=peer, device_id_type=MESH_ID)
-
-    barrier = pltpu.get_barrier_semaphore()
-    for peer in (core_peer, x_peer, y_peer):
-        pl.semaphore_signal(barrier, inc=1, device_id=peer, device_id_type=MESH_ID)
-    pl.semaphore_wait(barrier, 3)
-
-    swaps = []
     for c in range(CHUNKS):
-        src = a_ref.at[:, pl.ds(pl.multiple_of((1 - q) * half + c * step, step), step)]
-        swaps.append(copy(src, r_ref.at[:, pl.ds(c * step, step)], es.at[c], er.at[c], y_peer))
-        swaps[-1].start()
-    top = a_ref.at[:, pl.ds(0, total)]
-    h_y = copy(top, h_ref.at[q], hs.at[0], hr.at[1], y_peer)
-    h_x0 = copy(top, h_ref.at[q], hs.at[1], hr.at[0], x_peer)
-    h_c0 = copy(top, h_ref.at[q], hs.at[2], hr.at[0], core_peer)
-    h_x1 = copy(h_ref.at[1 - q], h_ref.at[1 - q], hs.at[3], hr.at[1], x_peer)
-    h_c1 = copy(h_ref.at[1 - q], h_ref.at[1 - q], hs.at[4], hr.at[1], core_peer)
-    f_c0 = copy(h_ref.at[q], h_ref.at[q], hs.at[2], hr.at[0], core_peer)
+        near[c].wait_send()
+        far[c].wait()
+
+    @pl.when(first_dev)
+    def _():
+        w_y.wait_send()
+        w_x0.wait_send()
+        w_c0.wait_send()
+
+    @pl.when(relay_dev)
+    def _():
+        w_x1.wait_send()
+        w_c1.wait_send()
+
+    @pl.when(row == 2)
+    def _():
+        w_c1.wait_send()
+
+    @pl.when(core == 0)
+    def _():
+        own_b.wait_send()
+        own_o.wait_send()
+        x_c.wait_send()
+        h_clo.wait_send()
+        h_chi.wait_send()
 
     @pl.when(row == 0)
     def _():
-        h_x0.start()
-        h_c0.start()
-        h_ref[q] = a_ref[:, 0:total]
-
-    s_ref[...] = jnp.zeros_like(s_ref)
-
-    def own(i, carry):
-        tile = a_ref[:, pl.ds(pl.multiple_of(i * 256, 256), 256)]
-        s_ref[0:width] += dot(tile, tile, 1, 1)
-        return carry
-
-    lax.fori_loop(0, rows // 256, own, 0)
+        h_xlo.wait_send()
 
     @pl.when(row == 2)
     def _():
-        h_x0.wait_recv()
-        f_c0.start()
-
-    own_c = copy(s_ref.at[pl.ds(0, width)], in1, ds.at[0], dr.at[0], core_peer)
-    own_x = copy(acc.at[0], in2.at[0], ds.at[1], dr.at[1], x_peer)
-    own_y = copy(f_ref.at[q], f_ref.at[q], ds.at[2], dr.at[2], y_peer)
-    own_b = copy(f_ref.at[q], f_ref.at[q], ds.at[3], dr.at[3], core_peer)
-    own_o = copy(f_ref.at[1 - q], f_ref.at[1 - q], ds.at[4], dr.at[4], core_peer)
+        h_xhi.wait_send()
 
     @pl.when(core == 1)
     def _():
-        own_c.start()
-
-    @pl.when(core == 0)
-    def _():
-        own_c.wait_recv()
-        acc[0] = s_ref[0:width] + in1[...]
-        own_x.start()
-        own_x.wait()
-        f_ref[q] = acc[0] + in2[0]
-        own_y.start()
-        own_b.start()
-
-    @pl.when(row == 0)
-    def _():
-        h_y.start()
-
-    first = q == 0
-    for c in range(CHUNKS):
-        swaps[c].wait_recv()
-        mine = a_ref[:, pl.ds(pl.multiple_of(q * half + c * step, step), step)]
-        other = r_ref[:, c * step:(c + 1) * step]
-        s_ref[width:] += dot(jnp.where(first, mine, other), jnp.where(first, other, mine), 1, 1)
-
-    x_c = copy(s_ref.at[pl.ds(width, width)], in1, ds.at[0], dr.at[0], core_peer)
-    x_y = copy(acc.at[0], in2.at[0], ds.at[1], dr.at[1], y_peer)
-    x_x = copy(acc.at[1], in2.at[1], ds.at[2], dr.at[2], x_peer)
-    x_b = copy(f_ref.at[2], f_ref.at[2], ds.at[5], dr.at[5], core_peer)
-
-    @pl.when(core == 0)
-    def _():
-        x_c.start()
-
-    @pl.when(core == 1)
-    def _():
-        own_c.wait_send()
-        x_c.wait_recv()
-        acc[0] = s_ref[width:] + in1[...]
-        x_y.start()
-        x_y.wait()
-        acc[1] = acc[0] + in2[0]
-        x_x.start()
-        x_x.wait()
-        f_ref[2] = acc[1] + in2[1]
-        x_b.start()
         x_b.wait_send()
-        own_b.wait_recv()
-        own_o.wait_recv()
-
-    @pl.when(core == 0)
-    def _():
-        own_y.wait()
-        own_o.start()
-        own_b.wait_send()
-        x_c.wait_send()
-
-    @pl.when(row == 0)
-    def _():
-        h_y.wait()
-        h_x1.start()
-        h_c1.start()
-        h_x0.wait_send()
-        h_c0.wait_send()
-        h_x1.wait_send()
-        h_c1.wait_send()
-
-    @pl.when(row == 2)
-    def _():
-        h_x1.wait_recv()
-        h_c1.start()
-        f_c0.wait_send()
-        h_c1.wait_send()
-
-    @pl.when(core == 1)
-    def _():
-        h_c0.wait_recv()
-        h_c1.wait_recv()
-
-    @pl.when(core == 0)
-    def _():
-        own_o.wait_send()
-        x_b.wait_recv()
-
-    for c in range(CHUNKS):
-        swaps[c].wait_send()
-
-
-def joint_kernel(count, width, a_ref, top_out, xi_out, t_ref, tau_ref, ok_ref, r_ref, *rest):
-    sums, sems, scratch = rest[:6], rest[6:12], rest[12:]
-    sums_kernel(a_ref, r_ref, *sums, *sems)
-    factor_kernel(count, width, lax.axis_index('col'), sums[0], sums[1], top_out, xi_out, t_ref, tau_ref, ok_ref, *scratch)
 
 
 def joint_call(a2, count, width):
@@ -395,7 +513,7 @@
     blocks = jax.ShapeDtypeStruct((2, count, width, width), f32)
     return pl.pallas_call(
         functools.partial(joint_kernel, count, width),
-        out_shape=(blocks, blocks, jax.ShapeDtypeStruct((2, width, width), f32), jax.ShapeDtypeStruct((2, 1, width), f32), jax.ShapeDtypeStruct((8, 128), f32), jax.ShapeDtypeStruct((cols, rows // 2), f32)),
+        out_shape=(blocks, blocks, jax.ShapeDtypeStruct((2, width, width), f32), jax.ShapeDtypeStruct((2, 1, width), f32), jax.ShapeDtypeStruct((8, 128), f32), jax.ShapeDtypeStruct((cols, rows), f32)),
         in_specs=[vmem],
         out_specs=(vmem,) * 6,
         scratch_shapes=[
@@ -405,7 +523,8 @@
             pltpu.VMEM((cols, cols), f32),
             pltpu.VMEM((2, cols, cols), f32),
             pltpu.VMEM((2, cols, cols), f32),
-            dma((CHUNKS,)), dma((CHUNKS,)), dma((5,)), dma((2,)), dma((6,)), dma((6,)),
+            sq, pltpu.VMEM((3, width, width), f32), pltpu.VMEM((2, width, width), f32), pltpu.VMEM((width, TILE), f32),
+            dma((CHUNKS,)), dma((CHUNKS,)), dma((CHUNKS,)), dma((CHUNKS,)), dma((6,)), dma((3,)), dma((6,)), dma((6,)), dma((3,)), dma((3,)), dma((3,)), dma((1,)),
         ] + [grid] * 5 + [pltpu.VMEM((SUB, LANES), f32)] * 2 + [sq] * 8 + [
             pltpu.VMEM((count, 1, width), f32), pltpu.VMEM((count, width, 1), f32), pltpu.VMEM((1, width), f32),
         ],
@@ -413,46 +532,40 @@
     )(a2)
 
 
-def v_kernel(place, a_ref, near_ref, far_ref, xi_ref, top_ref, out_ref, x0_ref, x1_ref):
+def v_kernel(place, a_ref, r_ref, xi_ref, top_ref, out_ref, x0_ref, x1_ref):
     slots, count, width, _ = xi_ref.shape
-    half = near_ref.shape[1]
-    q, row = place[0], place[1]
     x0_ref[...] = jnp.concatenate([xi_ref[0, i].T for i in range(2)], axis=1)
     x1_ref[...] = jnp.concatenate([xi_ref[1, i].T for i in range(count)], axis=1)
 
-    def rows_of(far, base, c):
-        at = pl.multiple_of(base + c * 256, 256)
-        own = a_ref[:, pl.ds(at, 256)]
-        par = far[:, pl.ds(pl.multiple_of(c * 256, 256), 256)]
+    def step(c, carry):
+        at = pl.ds(pl.multiple_of(c * TILE, TILE), TILE)
+        own = a_ref[:, at]
+        par = r_ref[:, at]
         both = jnp.concatenate([own[:width], par[:width], own[width:], par[width:]], axis=0)
-        out_ref[:width, pl.ds(at, 256)] = dot(x0_ref[...], both[:2 * width])
-        out_ref[width:, pl.ds(at, 256)] = dot(x1_ref[...], both)
-
-    def step(c, carry):
-        rows_of(near_ref, q * half, c)
-        rows_of(far_ref, (1 - q) * half, c)
+        out_ref[:width, at] = dot(x0_ref[...], both[:2 * width])
+        out_ref[width:, at] = dot(x1_ref[...], both)
         return carry
 
-    lax.fori_loop(0, half // 256, step, 0)
-
-    @pl.when(row == 0)
+    lax.fori_loop(0, a_ref.shape[1] // TILE, step, 0)
+
+    @pl.when(place[0] == 0)
     def _():
         for s in range(slots):
             out_ref[s * width:(s + 1) * width, 0:count * width] = jnp.concatenate([top_ref[s, i].T for i in range(count)], axis=1)
 
 
-def v_call(place, a2, near, far, xi, top):
+def v_call(place, a2, mirror, xi, top):
     f32 = jnp.float32
     width = xi.shape[-1]
     vmem = pl.BlockSpec(memory_space=pltpu.VMEM)
     return pl.pallas_call(
         v_kernel,
         out_shape=jax.ShapeDtypeStruct(a2.shape, f32),
-        in_specs=[pl.BlockSpec(memory_space=pltpu.SMEM)] + [vmem] * 5,
+        in_specs=[pl.BlockSpec(memory_space=pltpu.SMEM)] + [vmem] * 4,
         out_specs=vmem,
         scratch_shapes=[pltpu.VMEM((width, 2 * width), f32), pltpu.VMEM((width, 4 * width), f32)],
         compiler_params=pltpu.CompilerParams(vmem_limit_bytes=24 * 1024 * 1024),
-    )(place, a2, near, far, xi, top)
+    )(place, a2, mirror, xi, top)
 
 
 def col_sum(x):
@@ -557,16 +670,13 @@
     def per_device(a_blk):
         loc_rows, loc_panels, width = a_blk.shape
         count = loc_panels * col_count
-        me_col = lax.axis_index('col')
         me_row = lax.axis_index('row')
-        half = loc_rows // 2
-        place = jnp.stack([me_col, me_row]).astype(jnp.int32)
+        place = me_row.astype(jnp.int32).reshape(1)
         a2 = a_blk.transpose(1, 2, 0).reshape(loc_panels * width, loc_rows)
-        far = lax.ppermute(lax.dynamic_slice_in_dim(a2, me_col * half, half, axis=1), 'col', [(0, 1), (1, 0)])
-        top, x_inv, t_mat, tau, bad, near = joint_call(a2, count, width)
+        top, x_inv, t_mat, tau, bad, mirror = joint_call(a2, count, width)
 
         def gram_plan():
-            v_all = v_call(place, a2, near, far, x_inv, top)
+            v_all = v_call(place, a2, mirror, x_inv, top)
             return v_all.reshape(loc_panels, width, loc_rows).transpose(2, 0, 1), tau[:, 0], t_mat
 
         def safe_plan():

time: 206 us -> 163 us (0.79)
  Pallas kernels: 195 us -> 159 us
  starting transfers between devices: 3.39 us -> 0 us
    pallas_call x1, Pallas kernels: 181 us -> 145 us  [joint_call(): pl.pallas_call(functools.partial(joint_kernel, count, width), out_shape=(...]
    ppermute x1 -> x0, starting transfers between devices: 3.39 us -> none  [per_device(): lax.ppermute(lax.dynamic_slice_in_dim(a2, me_col * half, half, axis=1), '...]
  transfers between devices with their start and end apart: 1 -> 0, of which waited for: 0 -> 0; matrix products, arithmetic and copies ran while one was open for 1% -> 0% of each run, Pallas kernels for 89% -> 0%
where the time goes in v2:
time: 163 us
  Pallas kernels  159 us (98%)
  local copies, waits for them, and re-layouts  2.29 us (1%)
    pallas_call x1, Pallas kernels, joint_call(): pl.pallas_call(functools.partial(joint_kernel, count, width), out_shape=(...  145 us
    pallas_call x1, Pallas kernels, v_call(): pl.pallas_call(v_kernel, out_shape=jax.ShapeDtypeStruct(a2.shape, f32), i...  14.7 us

profile of v2, /device:TPU:0, one launch (start us, length us, event | category | flops | bytes accessed | tf_op | source)
XLA Modules:
  0.0 163.1 jit_solution(310302689568413113)
XLA Ops:
  0.6 144.5 %shard_map.38 = (f32[2,4,192,192]{3,2,1,0:T(8,128)}, f32[2,4,192,192]{3,2,1,0:T(8,128)}, f32[2,192,192]{2,1,0:T(8,128)}, f32[2,1,192]{2,1,0:T(1,128)S(1)}, f32[8,128]{1,0:T(8,128)S(1)}, /*index=5*/f32[384,2048]{1,0:T(8,128)}) custom-call(f32[384,2048]{1,0:T(8,128)} %bitcast.87), custom_call_target="tpu_custom_call" | custom-call | tf_op jit(solution)/shard_map/pallas_call | solution.py:514
  145.2 0.5 slice.40
  146.3 14.9 %conditional.1 = (f32[2048,2,192]{0,2,1:T(8,128)}, f32[2,192]{1,0:T(2,128)S(1)}, f32[2,192,192]{2,1,0:T(8,128)}) conditional(s32[]{:T(128)} %bitcast.6, (f32[8,128]{1,0:T(8,128)S(1)}, f32[2048,2,192]{0,2,1:T(8,128)}) %tuple.69, (s32[]{:T(128)}, f32[384,2048]{1,0:T(8,128)}, f32[384,2048]{1,0:T(8,128)}, f32[2,4,192,192]{3,2,1,0:T(8,128)}, ...), branch_computations={%region_0.10_spmd, %region_10.11_spmd} | conditional | flops 4716988416 | bytes 102292544 | solution.py:685
  146.6 14.7 %branch_1_fun.1 = f32[384,2048]{1,0:T(8,128)} custom-call(s32[1]{0:T(128)} %bitcast.1.place, f32[384,2048]{1,0:T(8,128)} %get-tuple-element.490.a_ref, f32[384,2048]{1,0:T(8,128)} %get-tuple-element.491.r_ref, f32[2,4,192,192]{3,2,1,0:T(8,128)} %get-tuple-element.492.xi_ref, f32[2,4,192,192]{3,2,1,0:T(8,128)} %get-tuple-element.493.top_ref), custom_call_target="tpu_custom_call" | custom-call | tf_op jit(solution)/shard_map/cond/branch_1_fun/pallas_call | solution.py:561
  161.3 0.0 copy-start.4
  161.3 1.8 %copy.52 = f32[2,192,192]{2,1,0:T(8,128)} copy(f32[2,192,192]{2,1,0:T(8,128)} %get-tuple-element.1030) | data formatting | bytes 589824
  163.1 0.0 copy-done.4
  (1 shorter events, 0.0 us)
Async XLA Ops:
  161.3 1.8 %copy-start.4 = (f32[2,192]{1,0:T(2,128)}, f32[2,192]{1,0:T(2,128)S(1)}, u32[]{:S(2)}) copy-start(f32[2,192]{1,0:T(2,128)S(1)} %get-tuple-element.1029) | copy-start | bytes 4612

commit v3 on v2

--- a/solution.py
+++ b/solution.py
@@ -114,7 +114,9 @@
 
 MESH_ID = pl.DeviceIdType.MESH
 CHUNKS = 4
+EARLY = 2
 TILE = 256
+V_LIMIT = 24
 
 
 def joint_kernel(count, width, a_ref, top_out, xi_out, t_ref, tau_ref, ok_ref, r_ref, f_ref, h_ref, s_ref, in1, in2, acc, p_ref, p_in, gd_ref, wp_ref,
@@ -163,7 +165,8 @@
         near.append(copy(a_ref.at[:, at], r_ref.at[:, at], es.at[c], er.at[c], y_peer))
         at = pl.ds(pl.multiple_of(q * half + c * step, step), step)
         far.append(copy(a_ref.at[:, at], r_ref.at[:, at], zs.at[c], zr.at[c], y_peer))
-    near[0].start()
+    for c in range(EARLY):
+        near[c].start()
 
     lo, hi = pl.ds(0, cols), pl.ds(cols, cols)
     h_x0 = copy(a_ref.at[:, pl.ds(0, total)], h_ref.at[q], hs.at[0], hr.at[0], x_peer)
@@ -211,7 +214,7 @@
     p_x.wait()
     gd_ref[q] = p_in[2] + p_in[1]
     p_y.start()
-    for c in range(1, CHUNKS):
+    for c in range(EARLY, CHUNKS):
         near[c].start()
 
     @pl.when(relay_dev)
@@ -233,9 +236,10 @@
     own_b = copy(f_ref.at[q], f_ref.at[q], ds.at[3], dr.at[3], core_peer)
     own_o = copy(f_ref.at[1 - q], f_ref.at[1 - q], ds.at[4], dr.at[4], core_peer)
     x_c = copy(s_ref.at[pl.ds(cols, cols)], in1, ds.at[0], dr.at[0], core_peer)
-    x_y = copy(acc.at[0], in2.at[0], ds.at[1], dr.at[1], y_peer)
-    x_x = copy(acc.at[1], in2.at[1], ds.at[2], dr.at[2], x_peer)
-    x_b = copy(f_ref.at[2], f_ref.at[2], ds.at[5], dr.at[5], core_peer)
+    parts = [pl.ds(0, width), pl.ds(width, width)]
+    x_y = [copy(acc.at[0, p], in2.at[0, p], ds.at[1 + 5 * i], dr.at[1 + 5 * i], y_peer) for i, p in enumerate(parts)]
+    x_x = [copy(acc.at[1, p], in2.at[1, p], ds.at[2 + 5 * i], dr.at[2 + 5 * i], x_peer) for i, p in enumerate(parts)]
+    x_b = [copy(f_ref.at[2, p], f_ref.at[2, p], ds.at[5 + 3 * i], dr.at[5 + 3 * i], core_peer) for i, p in enumerate(parts)]
 
     @pl.when(row == 0)
     def _():
@@ -295,13 +299,16 @@
             own_c.wait_send()
             x_c.wait_recv()
             acc[0] = s_ref[cols:] + in1[...]
-            x_y.start()
-            x_y.wait()
-            acc[1] = acc[0] + in2[0]
-            x_x.start()
-            x_x.wait()
-            f_ref[2] = acc[1] + in2[1]
-            x_b.start()
+            for i in range(2):
+                x_y[i].start()
+            for i, p in enumerate(parts):
+                x_y[i].wait()
+                acc[1, p] = acc[0, p] + in2[0, p]
+                x_x[i].start()
+            for i, p in enumerate(parts):
+                x_x[i].wait()
+                f_ref[2, p] = acc[1, p] + in2[1, p]
+                x_b[i].start()
 
         @pl.when(core == 0)
         def _():
@@ -329,7 +336,8 @@
 
         @pl.when(core == 0)
         def _():
-            x_b.wait_recv()
+            for i in range(2):
+                x_b[i].wait_recv()
 
         @pl.when(core == 1)
         def _():
@@ -500,7 +508,8 @@
 
     @pl.when(core == 1)
     def _():
-        x_b.wait_send()
+        for i in range(2):
+            x_b[i].wait_send()
 
 
 def joint_call(a2, count, width):
@@ -524,7 +533,7 @@
             pltpu.VMEM((2, cols, cols), f32),
             pltpu.VMEM((2, cols, cols), f32),
             sq, pltpu.VMEM((3, width, width), f32), pltpu.VMEM((2, width, width), f32), pltpu.VMEM((width, TILE), f32),
-            dma((CHUNKS,)), dma((CHUNKS,)), dma((CHUNKS,)), dma((CHUNKS,)), dma((6,)), dma((3,)), dma((6,)), dma((6,)), dma((3,)), dma((3,)), dma((3,)), dma((1,)),
+            dma((CHUNKS,)), dma((CHUNKS,)), dma((CHUNKS,)), dma((CHUNKS,)), dma((6,)), dma((3,)), dma((9,)), dma((9,)), dma((3,)), dma((3,)), dma((3,)), dma((1,)),
         ] + [grid] * 5 + [pltpu.VMEM((SUB, LANES), f32)] * 2 + [sq] * 8 + [
             pltpu.VMEM((count, 1, width), f32), pltpu.VMEM((count, width, 1), f32), pltpu.VMEM((1, width), f32),
         ],
@@ -532,39 +541,48 @@
     )(a2)
 
 
-def v_kernel(place, a_ref, r_ref, xi_ref, top_ref, out_ref, x0_ref, x1_ref):
+def v_kernel(place, a_ref, r_ref, xi_ref, top_ref, out_ref, x0_ref, x1_ref, head_ref):
     slots, count, width, _ = xi_ref.shape
-    x0_ref[...] = jnp.concatenate([xi_ref[0, i].T for i in range(2)], axis=1)
-    x1_ref[...] = jnp.concatenate([xi_ref[1, i].T for i in range(count)], axis=1)
-
-    def step(c, carry):
-        at = pl.ds(pl.multiple_of(c * TILE, TILE), TILE)
-        own = a_ref[:, at]
-        par = r_ref[:, at]
-        both = jnp.concatenate([own[:width], par[:width], own[width:], par[width:]], axis=0)
-        out_ref[:width, at] = dot(x0_ref[...], both[:2 * width])
-        out_ref[width:, at] = dot(x1_ref[...], both)
-        return carry
-
-    lax.fori_loop(0, a_ref.shape[1] // TILE, step, 0)
-
-    @pl.when(place[0] == 0)
+    c = pl.program_id(0)
+    is_head = jnp.logical_and(place[0] == 0, c < count * width // TILE)
+
+    @pl.when(c == 0)
+    def _():
+        x0_ref[...] = jnp.concatenate([xi_ref[0, i].T for i in range(2)], axis=1)
+        x1_ref[...] = jnp.concatenate([xi_ref[1, i].T for i in range(count)], axis=1)
+
+    @pl.when(jnp.logical_and(place[0] == 0, c == 0))
     def _():
         for s in range(slots):
-            out_ref[s * width:(s + 1) * width, 0:count * width] = jnp.concatenate([top_ref[s, i].T for i in range(count)], axis=1)
+            head = jnp.concatenate([top_ref[s, i].T for i in range(count)], axis=1)
+            for t in range(count * width // TILE):
+                head_ref[t, s * width:(s + 1) * width] = head[:, t * TILE:(t + 1) * TILE]
+
+    @pl.when(is_head)
+    def _():
+        out_ref[...] = head_ref[jnp.minimum(c, count * width // TILE - 1)]
+
+    @pl.when(jnp.logical_not(is_head))
+    def _():
+        both = jnp.concatenate([a_ref[:width], r_ref[:width], a_ref[width:], r_ref[width:]], axis=0)
+        out_ref[:width] = dot(x0_ref[...], both[:2 * width])
+        out_ref[width:] = dot(x1_ref[...], both)
 
 
 def v_call(place, a2, mirror, xi, top):
     f32 = jnp.float32
+    cols, rows = a2.shape
     width = xi.shape[-1]
-    vmem = pl.BlockSpec(memory_space=pltpu.VMEM)
+    tile = pl.BlockSpec((cols, TILE), lambda c: (0, c))
+    whole = pl.BlockSpec(memory_space=pltpu.VMEM)
     return pl.pallas_call(
         v_kernel,
+        grid=(rows // TILE,),
         out_shape=jax.ShapeDtypeStruct(a2.shape, f32),
-        in_specs=[pl.BlockSpec(memory_space=pltpu.SMEM)] + [vmem] * 4,
-        out_specs=vmem,
-        scratch_shapes=[pltpu.VMEM((width, 2 * width), f32), pltpu.VMEM((width, 4 * width), f32)],
-        compiler_params=pltpu.CompilerParams(vmem_limit_bytes=24 * 1024 * 1024),
+        in_specs=[pl.BlockSpec(memory_space=pltpu.SMEM), tile, tile, whole, whole],
+        out_specs=tile,
+        scratch_shapes=[pltpu.VMEM((width, 2 * width), f32), pltpu.VMEM((width, 4 * width), f32), pltpu.VMEM((4 * width // TILE, cols, TILE), f32)],
+        compiler_params=pltpu.CompilerParams(vmem_limit_bytes=V_LIMIT * 1024 * 1024),
     )(place, a2, mirror, xi, top)
 
 

time: 163 us -> 157 us (0.963); the launches traced: 163 us -> 154 us
  Pallas kernels: 159 us -> 150 us
    pallas_call x1, Pallas kernels: 145 us -> 139 us  [joint_call(): pl.pallas_call(functools.partial(joint_kernel, count, width), out_shape=(...]
    pallas_call x1, Pallas kernels: 14.7 us -> 11.8 us  [v_call(): pl.pallas_call(v_kernel, grid=(rows // TILE,), out_shape=jax.ShapeDtypeSt...]
where the time goes in v3:
time: 157 us; the launch traced here: 154 us
  Pallas kernels  150 us (96%)
  local copies, waits for them, and re-layouts  2.29 us (1%)
    pallas_call x1, Pallas kernels, joint_call(): pl.pallas_call(functools.partial(joint_kernel, count, width), out_shape=(...  139 us
    pallas_call x1, Pallas kernels, v_call(): pl.pallas_call(v_kernel, grid=(rows // TILE,), out_shape=jax.ShapeDtypeSt...  11.8 us

profile of v3, /device:TPU:0, one launch (start us, length us, event | category | flops | bytes accessed | tf_op | source)
XLA Modules:
  0.0 154.2 jit_solution(263868441981696718)
XLA Ops:
  0.6 138.6 %shard_map.38 = (f32[2,4,192,192]{3,2,1,0:T(8,128)}, f32[2,4,192,192]{3,2,1,0:T(8,128)}, f32[2,192,192]{2,1,0:T(8,128)}, f32[2,1,192]{2,1,0:T(1,128)S(1)}, f32[8,128]{1,0:T(8,128)S(1)}, /*index=5*/f32[384,2048]{1,0:T(8,128)}) custom-call(f32[384,2048]{1,0:T(8,128)} %bitcast.87), custom_call_target="tpu_custom_call" | custom-call | tf_op jit(solution)/shard_map/pallas_call | solution.py:523
  139.3 0.5 slice.40
  140.4 12.0 %conditional.1 = (f32[2048,2,192]{0,2,1:T(8,128)}, f32[2,192]{1,0:T(2,128)S(1)}, f32[2,192,192]{2,1,0:T(8,128)}) conditional(s32[]{:T(128)} %bitcast.6, (f32[8,128]{1,0:T(8,128)S(1)}, f32[2048,2,192]{0,2,1:T(8,128)}) %tuple.69, (s32[]{:T(128)}, f32[384,2048]{1,0:T(8,128)}, f32[384,2048]{1,0:T(8,128)}, f32[2,4,192,192]{3,2,1,0:T(8,128)}, ...), branch_computations={%region_0.10_spmd, %region_10.11_spmd} | conditional | flops 4716988416 | bytes 102292544 | solution.py:703
  140.7 11.8 %branch_1_fun.1 = f32[384,2048]{1,0:T(8,128)} custom-call(s32[1]{0:T(128)} %bitcast.1.place, f32[384,2048]{1,0:T(8,128)} %get-tuple-element.490.a_ref, f32[384,2048]{1,0:T(8,128)} %get-tuple-element.491.r_ref, f32[2,4,192,192]{3,2,1,0:T(8,128)} %get-tuple-element.492.xi_ref, f32[2,4,192,192]{3,2,1,0:T(8,128)} %get-tuple-element.493.top_ref), custom_call_target="tpu_custom_call" | custom-call | tf_op jit(solution)/shard_map/cond/branch_1_fun/pallas_call | solution.py:578
  152.4 0.0 copy-start.4
  152.4 1.8 %copy.52 = f32[2,192,192]{2,1,0:T(8,128)} copy(f32[2,192,192]{2,1,0:T(8,128)} %get-tuple-element.1030) | data formatting | bytes 589824
  154.2 0.0 copy-done.4
  (1 shorter events, 0.0 us)
Async XLA Ops:
  152.4 1.8 %copy-start.4 = (f32[2,192]{1,0:T(2,128)}, f32[2,192]{1,0:T(2,128)S(1)}, u32[]{:S(2)}) copy-start(f32[2,192]{1,0:T(2,128)S(1)} %get-tuple-element.1029) | copy-start | bytes 4612

commit v4 on v3

--- a/solution.py
+++ b/solution.py
@@ -190,6 +190,7 @@
     p_c = copy(p_ref, p_in.at[0], ps.at[0], pr.at[0], core_peer)
     p_x = copy(p_in.at[2], p_in.at[1], ps.at[1], pr.at[1], x_peer)
     p_y = copy(gd_ref.at[q], gd_ref.at[q], ps.at[2], pr.at[2], y_peer)
+    p_b = copy(gd_ref.at[1 - q], gd_ref.at[1 - q], ps.at[3], pr.at[3], core_peer)
     p_c.start()
 
     s_ref[...] = jnp.zeros_like(s_ref)
@@ -197,7 +198,7 @@
 
     def own(i, carry):
         tile = a_ref[:, pl.ds(pl.multiple_of(i * TILE, TILE), TILE)]
-        s_ref[0:cols] += dot(tile, tile, 1, 1)
+        s_ref[width:cols] += dot(tile[width:], tile, 1, 1)
         return carry
 
     p_c.wait()
@@ -213,7 +214,11 @@
     lax.fori_loop(0, rows // TILE // 2, own, 0)
     p_x.wait()
     gd_ref[q] = p_in[2] + p_in[1]
-    p_y.start()
+
+    @pl.when(core == 0)
+    def _():
+        p_y.start()
+
     for c in range(EARLY, CHUNKS):
         near[c].start()
 
@@ -230,11 +235,12 @@
 
     lax.fori_loop(rows // TILE // 2, rows // TILE, own, 0)
 
-    own_c = copy(s_ref.at[pl.ds(0, cols)], in1, ds.at[0], dr.at[0], core_peer)
-    own_x = copy(acc.at[0], in2.at[0], ds.at[1], dr.at[1], x_peer)
-    own_y = copy(f_ref.at[q], f_ref.at[q], ds.at[2], dr.at[2], y_peer)
-    own_b = copy(f_ref.at[q], f_ref.at[q], ds.at[3], dr.at[3], core_peer)
-    own_o = copy(f_ref.at[1 - q], f_ref.at[1 - q], ds.at[4], dr.at[4], core_peer)
+    low = pl.ds(width, width)
+    own_c = copy(s_ref.at[low], in1.at[low], ds.at[0], dr.at[0], core_peer)
+    own_x = copy(acc.at[0, low], in2.at[0, low], ds.at[1], dr.at[1], x_peer)
+    own_y = copy(f_ref.at[q, low], f_ref.at[q, low], ds.at[2], dr.at[2], y_peer)
+    own_b = copy(f_ref.at[q, low], f_ref.at[q, low], ds.at[3], dr.at[3], core_peer)
+    own_o = copy(f_ref.at[1 - q, low], f_ref.at[1 - q, low], ds.at[4], dr.at[4], core_peer)
     x_c = copy(s_ref.at[pl.ds(cols, cols)], in1, ds.at[0], dr.at[0], core_peer)
     parts = [pl.ds(0, width), pl.ds(width, width)]
     x_y = [copy(acc.at[0, p], in2.at[0, p], ds.at[1 + 5 * i], dr.at[1 + 5 * i], y_peer) for i, p in enumerate(parts)]
@@ -256,7 +262,15 @@
         own_c.start()
         w_c0.wait_recv()
 
-    p_y.wait()
+    @pl.when(core == 0)
+    def _():
+        p_y.wait()
+        p_b.start()
+
+    @pl.when(core == 1)
+    def _():
+        p_b.wait_recv()
+
     g_ref[0, 0] = gd_ref[0]
     w_ref[0, 0] = wp_ref[:, 0:width].T
 
@@ -270,14 +284,14 @@
         @pl.when(core == 0)
         def _():
             own_c.wait_recv()
-            acc[0] = s_ref[0:cols] + in1[...]
+            acc[0, low] = s_ref[low] + in1[low]
             own_x.start()
 
     def own_stage2():
         @pl.when(core == 0)
         def _():
             own_x.wait()
-            f_ref[q] = acc[0] + in2[0]
+            f_ref[q, low] = acc[0, low] + in2[0, low]
             own_y.start()
             own_b.start()
 
@@ -305,10 +319,6 @@
                 x_y[i].wait()
                 acc[1, p] = acc[0, p] + in2[0, p]
                 x_x[i].start()
-            for i, p in enumerate(parts):
-                x_x[i].wait()
-                f_ref[2, p] = acc[1, p] + in2[1, p]
-                x_b[i].start()
 
         @pl.when(core == 0)
         def _():
@@ -334,11 +344,6 @@
             h_clo.start()
             h_c2.wait_send()
 
-        @pl.when(core == 0)
-        def _():
-            for i in range(2):
-                x_b[i].wait_recv()
-
         @pl.when(core == 1)
         def _():
             h_c0.wait_recv()
@@ -347,23 +352,36 @@
             own_b.wait_recv()
             own_o.wait_recv()
 
+        for i in range(count):
+            for j in range(count):
+                if i + j > 0:
+                    sj = j // 2 * width
+                    w_ref[i, j] = h_ref[j % 2, sj:sj + width, i * width:(i + 1) * width].T
+        for i in range(2):
+            g_ref[i, i + 2] = f_ref[i, low, 0:width].T
+            g_ref[i + 2, i + 2] = f_ref[i, low, width:]
+            diag_of(i + 2, g_ref[i + 2, i + 2])
+        g_ref[1, 1] = gd_ref[1]
+        diag_of(1, gd_ref[1])
+
+        @pl.when(core == 1)
+        def _():
+            for i, p in enumerate(parts):
+                x_x[i].wait()
+                f_ref[2, p] = acc[1, p] + in2[1, p]
+                x_b[i].start()
+
+        @pl.when(core == 0)
+        def _():
+            for i in range(2):
+                x_b[i].wait_recv()
+
         for c in range(CHUNKS):
             far[c].start()
-        for i in range(count):
-            qi, si = i % 2, i // 2 * width
-            for j in range(count):
-                qj, sj = j % 2, j // 2 * width
-                if i + j > 0:
-                    w_ref[i, j] = h_ref[qj, sj:sj + width, i * width:(i + 1) * width].T
-                    if i <= j:
-                        if qi == qj:
-                            g_ref[i, j] = f_ref[qi, si:si + width, sj:sj + width]
-                        elif qi == 0:
-                            g_ref[i, j] = f_ref[2, si:si + width, sj:sj + width]
-                        else:
-                            g_ref[i, j] = f_ref[2, sj:sj + width, si:si + width].T
-            if i > 0:
-                diag_of(i, g_ref[i, i])
+        g_ref[0, 1] = f_ref[2, 0:width, 0:width]
+        g_ref[0, 3] = f_ref[2, 0:width, width:]
+        g_ref[1, 2] = f_ref[2, width:, 0:width].T
+        g_ref[2, 3] = f_ref[2, width:, width:]
 
     def panel(j, bad):
         gs[...] = g_ref[j, j]
@@ -492,6 +510,7 @@
 
     @pl.when(core == 0)
     def _():
+        p_b.wait_send()
         own_b.wait_send()
         own_o.wait_send()
         x_c.wait_send()
@@ -533,7 +552,7 @@
             pltpu.VMEM((2, cols, cols), f32),
             pltpu.VMEM((2, cols, cols), f32),
             sq, pltpu.VMEM((3, width, width), f32), pltpu.VMEM((2, width, width), f32), pltpu.VMEM((width, TILE), f32),
-            dma((CHUNKS,)), dma((CHUNKS,)), dma((CHUNKS,)), dma((CHUNKS,)), dma((6,)), dma((3,)), dma((9,)), dma((9,)), dma((3,)), dma((3,)), dma((3,)), dma((1,)),
+            dma((CHUNKS,)), dma((CHUNKS,)), dma((CHUNKS,)), dma((CHUNKS,)), dma((6,)), dma((3,)), dma((9,)), dma((9,)), dma((4,)), dma((4,)), dma((3,)), dma((1,)),
         ] + [grid] * 5 + [pltpu.VMEM((SUB, LANES), f32)] * 2 + [sq] * 8 + [
             pltpu.VMEM((count, 1, width), f32), pltpu.VMEM((count, width, 1), f32), pltpu.VMEM((1, width), f32),
         ],
@@ -541,13 +560,14 @@
     )(a2)
 
 
-def v_kernel(place, a_ref, r_ref, xi_ref, top_ref, out_ref, x0_ref, x1_ref, head_ref):
+def v_kernel(place, a_ref, r_ref, xi_ref, top_ref, t_ref, out_ref, t_out, x0_ref, x1_ref, head_ref):
     slots, count, width, _ = xi_ref.shape
     c = pl.program_id(0)
     is_head = jnp.logical_and(place[0] == 0, c < count * width // TILE)
 
     @pl.when(c == 0)
     def _():
+        t_out[...] = t_ref[...]
         x0_ref[...] = jnp.concatenate([xi_ref[0, i].T for i in range(2)], axis=1)
         x1_ref[...] = jnp.concatenate([xi_ref[1, i].T for i in range(count)], axis=1)
 
@@ -569,7 +589,7 @@
         out_ref[width:] = dot(x1_ref[...], both)
 
 
-def v_call(place, a2, mirror, xi, top):
+def v_call(place, a2, mirror, xi, top, t_mat):
     f32 = jnp.float32
     cols, rows = a2.shape
     width = xi.shape[-1]
@@ -578,12 +598,12 @@
     return pl.pallas_call(
         v_kernel,
         grid=(rows // TILE,),
-        out_shape=jax.ShapeDtypeStruct(a2.shape, f32),
-        in_specs=[pl.BlockSpec(memory_space=pltpu.SMEM), tile, tile, whole, whole],
-        out_specs=tile,
+        out_shape=(jax.ShapeDtypeStruct(a2.shape, f32), jax.ShapeDtypeStruct(t_mat.shape, f32)),
+        in_specs=[pl.BlockSpec(memory_space=pltpu.SMEM), tile, tile, whole, whole, whole],
+        out_specs=(tile, pl.BlockSpec(t_mat.shape, lambda c: (0, 0, 0))),
         scratch_shapes=[pltpu.VMEM((width, 2 * width), f32), pltpu.VMEM((width, 4 * width), f32), pltpu.VMEM((4 * width // TILE, cols, TILE), f32)],
         compiler_params=pltpu.CompilerParams(vmem_limit_bytes=V_LIMIT * 1024 * 1024),
-    )(place, a2, mirror, xi, top)
+    )(place, a2, mirror, xi, top, t_mat)
 
 
 def col_sum(x):
@@ -694,8 +714,8 @@
         top, x_inv, t_mat, tau, bad, mirror = joint_call(a2, count, width)
 
         def gram_plan():
-            v_all = v_call(place, a2, mirror, x_inv, top)
-            return v_all.reshape(loc_panels, width, loc_rows).transpose(2, 0, 1), tau[:, 0], t_mat
+            v_all, t_own = v_call(place, a2, mirror, x_inv, top, t_mat)
+            return v_all.reshape(loc_panels, width, loc_rows).transpose(2, 0, 1), tau[:, 0], t_own
 
         def safe_plan():
             return column_plan(a_blk * jnp.minimum(bad[0, 0], 1.0), col_count)

time: 157 us -> 152 us (0.968)
  the two profiles are of different devices: /device:TPU:0 before, /device:TPU:2 now
where the time goes in v4:
time: 152 us
  Pallas kernels  149 us (98%)
    pallas_call x1, Pallas kernels, joint_call(): pl.pallas_call(functools.partial(joint_kernel, count, width), out_shape=(...  136 us
    pallas_call x1, Pallas kernels, v_call(): pl.pallas_call(v_kernel, grid=(rows // TILE,), out_shape=(jax.ShapeDtypeS...  12.6 us

profile of v4, /device:TPU:2, one launch (start us, length us, event | category | flops | bytes accessed | tf_op | source)
XLA Modules:
  0.0 151.5 jit_solution(5606736889502980080)
XLA Ops:
  0.6 136.3 %shard_map.38 = (f32[2,4,192,192]{3,2,1,0:T(8,128)}, f32[2,4,192,192]{3,2,1,0:T(8,128)}, f32[2,192,192]{2,1,0:T(8,128)}, f32[2,1,192]{2,1,0:T(1,128)S(1)}, f32[8,128]{1,0:T(8,128)S(1)}, /*index=5*/f32[384,2048]{1,0:T(8,128)}) custom-call(f32[384,2048]{1,0:T(8,128)} %bitcast.87), custom_call_target="tpu_custom_call" | custom-call | tf_op jit(solution)/shard_map/pallas_call | solution.py:542
  136.9 0.5 slice.40
  138.1 13.5 %conditional.1 = (f32[2048,2,192]{0,2,1:T(8,128)}, f32[2,192]{1,0:T(2,128)}, f32[2,192,192]{2,1,0:T(8,128)}) conditional(s32[]{:T(128)} %bitcast.6, (f32[8,128]{1,0:T(8,128)S(1)}, f32[2048,2,192]{0,2,1:T(8,128)}) %tuple.69, (s32[]{:T(128)}, f32[384,2048]{1,0:T(8,128)}, f32[384,2048]{1,0:T(8,128)}, f32[2,4,192,192]{3,2,1,0:T(8,128)}, ...), branch_computations={%region_0.10_spmd, %region_10.11_spmd} | conditional | flops 4716988416 | bytes 102298720 | solution.py:723
  138.3 12.6 %branch_1_fun.1 = (f32[384,2048]{1,0:T(8,128)}, f32[2,192,192]{2,1,0:T(8,128)}) custom-call(s32[1]{0:T(128)} %bitcast.1.place, f32[384,2048]{1,0:T(8,128)} %get-tuple-element.490.a_ref, f32[384,2048]{1,0:T(8,128)} %get-tuple-element.491.r_ref, f32[2,4,192,192]{3,2,1,0:T(8,128)} %get-tuple-element.492.xi_ref, f32[2,4,192,192]{3,2,1,0:T(8,128)} %get-tuple-element.493.top_ref, ...), custom_call_target="tpu_custom_call" | custom-call | tf_op jit(solution)/shard_map/cond/branch_1_fun/pallas_call | solution.py:598
  151.0 0.6 copy.12

commit v5 on v4

--- a/solution.py
+++ b/solution.py
@@ -113,13 +113,13 @@
 
 
 MESH_ID = pl.DeviceIdType.MESH
-CHUNKS = 4
-EARLY = 2
+CHUNKS = 8
+EARLY = 4
 TILE = 256
 V_LIMIT = 24
 
 
-def joint_kernel(count, width, a_ref, top_out, xi_out, t_ref, tau_ref, ok_ref, r_ref, f_ref, h_ref, s_ref, in1, in2, acc, p_ref, p_in, gd_ref, wp_ref,
+def joint_kernel(count, width, a_ref, top_out, xi_out, t_ref, tau_ref, ok_ref, r_out, r_ref, out_sem, f_ref, h_ref, s_ref, in1, in2, acc, p_ref, p_in, gd_ref, wp_ref,
                  es, er, zs, zr, hs, hr, ds, dr, ps, pr, ws, wr,
                  top_ref, xi_ref, g_ref, w_ref, x_ref, rb_ref, xb_ref, gs, bs, ri_s, vi_s, xi_s, rs, xs, vs, dg_ref, dc_ref, tau_s):
     cols, rows = a_ref.shape
@@ -295,6 +295,11 @@
             own_y.start()
             own_b.start()
 
+    def put_right(j, t, r_inv, v_inv):
+        r_row = dot(r_inv, g_ref[j, t], 0, 0)
+        top_ref[j, t] = r_row
+        x_ref[j, t] = dot(v_inv, w_ref[j, t] - r_row)
+
     def finish_sums():
         first = q == 0
         for c in range(CHUNKS):
@@ -363,6 +368,15 @@
             diag_of(i + 2, g_ref[i + 2, i + 2])
         g_ref[1, 1] = gd_ref[1]
         diag_of(1, gd_ref[1])
+        put_right(0, 2, ri_s[...], vi_s[...])
+
+        def early(i, carry):
+            top_ref[i, 0] = dot(w_ref[i, 0], xi_s[...])
+            w_ref[i, 2] -= dot(top_ref[i, 0], x_ref[0, 2])
+            return carry
+
+        lax.fori_loop(1, count, early, 0)
+        g_ref[2, 2] -= dot(top_ref[0, 2], top_ref[0, 2], 0, 0)
 
         @pl.when(core == 1)
         def _():
@@ -382,6 +396,8 @@
         g_ref[0, 3] = f_ref[2, 0:width, width:]
         g_ref[1, 2] = f_ref[2, width:, 0:width].T
         g_ref[2, 3] = f_ref[2, width:, width:]
+
+    r_copy = pltpu.make_async_copy(r_ref, r_out, out_sem)
 
     def panel(j, bad):
         gs[...] = g_ref[j, j]
@@ -429,26 +445,32 @@
         top_ref[j, j] = rs[...] + vs[...]
 
         def right(t, carry):
-            r_row = dot(r_inv, g_ref[j, t], 0, 0)
-            top_ref[j, t] = r_row
-            x_ref[j, t] = dot(v_inv, w_ref[j, t] - r_row)
+            @pl.when(jnp.logical_or(j != 0, t != 2))
+            def _():
+                put_right(j, t, r_inv, v_inv)
+
             return carry
 
         lax.fori_loop(j + 1, count, right, 0)
 
         def below(i, carry):
-            v_col = dot(w_ref[i, j], x_inv)
-            top_ref[i, j] = v_col
+            @pl.when(j != 0)
+            def _():
+                top_ref[i, j] = dot(w_ref[i, j], x_inv)
 
             def upd_w(t, c):
-                w_ref[i, t] -= dot(v_col, x_ref[j, t])
+                @pl.when(jnp.logical_or(j != 0, t != 2))
+                def _():
+                    w_ref[i, t] -= dot(top_ref[i, j], x_ref[j, t])
+
                 return c
 
             lax.fori_loop(j + 1, count, upd_w, 0)
-            r_i = top_ref[j, i]
-
             def upd_g(t, c):
-                g_ref[i, t] -= dot(r_i, top_ref[j, t], 0, 0)
+                @pl.when(jnp.logical_or(j != 0, jnp.logical_or(i != 2, t != 2)))
+                def _():
+                    g_ref[i, t] -= dot(top_ref[j, i], top_ref[j, t], 0, 0)
+
                 return c
 
             lax.fori_loop(i, count, upd_g, 0)
@@ -470,6 +492,12 @@
 
         size = lax.fori_loop(0, j + 1, coef, jnp.zeros((1, width), jnp.float32))
         slot = j // 2
+
+        @pl.when(j == count - 2)
+        def _():
+            for c in range(CHUNKS):
+                far[c].wait_recv()
+            r_copy.start()
 
         @pl.when(j % 2 == q)
         def _():
@@ -489,9 +517,10 @@
     bad = lax.fori_loop(0, count, panel, jnp.float32(0.0))
     ok_ref[...] = jnp.full(ok_ref.shape, bad, jnp.float32)
 
+    r_copy.wait()
     for c in range(CHUNKS):
         near[c].wait_send()
-        far[c].wait()
+        far[c].wait_send()
 
     @pl.when(first_dev)
     def _():
@@ -543,8 +572,10 @@
         functools.partial(joint_kernel, count, width),
         out_shape=(blocks, blocks, jax.ShapeDtypeStruct((2, width, width), f32), jax.ShapeDtypeStruct((2, 1, width), f32), jax.ShapeDtypeStruct((8, 128), f32), jax.ShapeDtypeStruct((cols, rows), f32)),
         in_specs=[vmem],
-        out_specs=(vmem,) * 6,
+        out_specs=(vmem,) * 5 + (pl.BlockSpec(memory_space=pl.ANY),),
         scratch_shapes=[
+            pltpu.VMEM((cols, rows), f32),
+            pltpu.SemaphoreType.DMA,
             pltpu.VMEM((3, cols, cols), f32),
             pltpu.VMEM((2, cols, 2 * cols), f32),
             pltpu.VMEM((2 * cols, cols), f32),

time: 152 us -> 147 us (0.967)
  the two profiles are of different devices: /device:TPU:2 before, /device:TPU:6 now
where the time goes in v5:
time: 147 us
  Pallas kernels  145 us (99%)
    pallas_call x1, Pallas kernels, joint_call(): pl.pallas_call(functools.partial(joint_kernel, count, width), out_shape=(...  132 us
    pallas_call x1, Pallas kernels, v_call(): pl.pallas_call(v_kernel, grid=(rows // TILE,), out_shape=(jax.ShapeDtypeS...  12.6 us

profile of v5, /device:TPU:6, one launch (start us, length us, event | category | flops | bytes accessed | tf_op | source)
XLA Modules:
  0.0 147.1 jit_solution(10672591288389451784)
XLA Ops:
  0.6 132.0 %shard_map.38 = (f32[2,4,192,192]{3,2,1,0:T(8,128)}, f32[2,4,192,192]{3,2,1,0:T(8,128)}, f32[2,192,192]{2,1,0:T(8,128)}, f32[2,1,192]{2,1,0:T(1,128)S(1)}, f32[8,128]{1,0:T(8,128)S(1)}, /*index=5*/f32[384,2048]{1,0:T(8,128)}) custom-call(f32[384,2048]{1,0:T(8,128)} %bitcast.87), custom_call_target="tpu_custom_call" | custom-call | tf_op jit(solution)/shard_map/pallas_call | solution.py:571
  132.7 0.5 slice.40
  133.8 13.2 %conditional.1 = (f32[2048,2,192]{0,2,1:T(8,128)}, f32[2,192]{1,0:T(2,128)}, f32[2,192,192]{2,1,0:T(8,128)}) conditional(s32[]{:T(128)} %bitcast.6, (f32[8,128]{1,0:T(8,128)S(1)}, f32[2048,2,192]{0,2,1:T(8,128)}) %tuple.69, (s32[]{:T(128)}, f32[384,2048]{1,0:T(8,128)}, f32[384,2048]{1,0:T(8,128)}, f32[2,4,192,192]{3,2,1,0:T(8,128)}, ...), branch_computations={%region_0.10_spmd, %region_10.11_spmd} | conditional | flops 4716988416 | bytes 102298720 | solution.py:754
  133.8 12.6 %branch_1_fun.1 = (f32[384,2048]{1,0:T(8,128)}, f32[2,192,192]{2,1,0:T(8,128)}) custom-call(s32[1]{0:T(128)} %bitcast.1.place, f32[384,2048]{1,0:T(8,128)} %get-tuple-element.490.a_ref, f32[384,2048]{1,0:T(8,128)} %get-tuple-element.491.r_ref, f32[2,4,192,192]{3,2,1,0:T(8,128)} %get-tuple-element.492.xi_ref, f32[2,4,192,192]{3,2,1,0:T(8,128)} %get-tuple-element.493.top_ref, ...), custom_call_target="tpu_custom_call" | custom-call | tf_op jit(solution)/shard_map/cond/branch_1_fun/pallas_call | solution.py:629
  146.5 0.6 copy.12

commit v6 on v5

--- a/solution.py
+++ b/solution.py
@@ -114,7 +114,7 @@
 
 MESH_ID = pl.DeviceIdType.MESH
 CHUNKS = 8
-EARLY = 4
+EARLY = 5
 TILE = 256
 V_LIMIT = 24
 

time: 147 us -> 146 us (level)
  the two profiles are of different devices: /device:TPU:6 before, /device:TPU:0 now
where the time goes in v6:
time: 146 us; the launch traced here: 145 us
  Pallas kernels  143 us (98%)
    pallas_call x1, Pallas kernels, joint_call(): pl.pallas_call(functools.partial(joint_kernel, count, width), out_shape=(...  131 us
    pallas_call x1, Pallas kernels, v_call(): pl.pallas_call(v_kernel, grid=(rows // TILE,), out_shape=(jax.ShapeDtypeS...  11.9 us

profile of v6, /device:TPU:0, one launch (start us, length us, event | category | flops | bytes accessed | tf_op | source)
XLA Modules:
  0.0 145.2 jit_solution(13606300354693864959)
XLA Ops:
  0.6 130.8 %shard_map.38 = (f32[2,4,192,192]{3,2,1,0:T(8,128)}, f32[2,4,192,192]{3,2,1,0:T(8,128)}, f32[2,192,192]{2,1,0:T(8,128)}, f32[2,1,192]{2,1,0:T(1,128)S(1)}, f32[8,128]{1,0:T(8,128)S(1)}, /*index=5*/f32[384,2048]{1,0:T(8,128)}) custom-call(f32[384,2048]{1,0:T(8,128)} %bitcast.87), custom_call_target="tpu_custom_call" | custom-call | tf_op jit(solution)/shard_map/pallas_call | solution.py:571
  131.5 0.5 slice.40
  132.7 12.5 %conditional.1 = (f32[2048,2,192]{0,2,1:T(8,128)}, f32[2,192]{1,0:T(2,128)}, f32[2,192,192]{2,1,0:T(8,128)}) conditional(s32[]{:T(128)} %bitcast.6, (f32[8,128]{1,0:T(8,128)S(1)}, f32[2048,2,192]{0,2,1:T(8,128)}) %tuple.69, (s32[]{:T(128)}, f32[384,2048]{1,0:T(8,128)}, f32[384,2048]{1,0:T(8,128)}, f32[2,4,192,192]{3,2,1,0:T(8,128)}, ...), branch_computations={%region_0.10_spmd, %region_10.11_spmd} | conditional | flops 4716988416 | bytes 102298720 | solution.py:754
  132.7 11.9 %branch_1_fun.1 = (f32[384,2048]{1,0:T(8,128)}, f32[2,192,192]{2,1,0:T(8,128)}) custom-call(s32[1]{0:T(128)} %bitcast.1.place, f32[384,2048]{1,0:T(8,128)} %get-tuple-element.490.a_ref, f32[384,2048]{1,0:T(8,128)} %get-tuple-element.491.r_ref, f32[2,4,192,192]{3,2,1,0:T(8,128)} %get-tuple-element.492.xi_ref, f32[2,4,192,192]{3,2,1,0:T(8,128)} %get-tuple-element.493.top_ref, ...), custom_call_target="tpu_custom_call" | custom-call | tf_op jit(solution)/shard_map/cond/branch_1_fun/pallas_call | solution.py:629
  144.6 0.6 copy.12
